TPU v7x, 512 devices: a whole 4x4x16 slice. The times are simulated.
512 devices in a mesh: gx: 4 (over y_hi, core), gy: 16 (over z), gz: 8 (over y_lo, x).
Axes of the slice: x: 4, y: 4 (y_hi: 2, y_lo: 2; y = y_hi * 2 + y_lo), z: 16, core: 2. Of those that a mesh axis runs over, the one named last changes fastest.
Arguments:
- heat_level_grid: float32 [256, 1024, 512], P('gz', 'gy', 'gx'), may hold values from -16 to 16, as said below
- interval_first_class: int32 [1], replicated, may hold values from 0 to 95
- interval_beyond_class: int32 [1], replicated, may hold values from 128 to 256
Outputs:
- magnitude: float32 [256, 1024, 512], P('gz', 'gy', 'gx')
- histogram: float32 [256], replicated
- stats: float32 [4], replicated
Inputs may be any that keep to these rules, and one draw needn't show every extreme that they name: `heat_level_grid`: each entry is a rough value times an amplitude that is constant on blocks of 8 x 4 x 4 cells (z, y, x) and varies over a factor of 16 between blocks.
All inputs are finite; a program needn't handle non-finite values.
Results may differ from a plain program's by a relative error of at most 0.0003.
Values sent between devices are 32-bit elements; how exact they have to be, the bound alone decides.
A program may use at most 64 MiB of HBM per device.

v0:
```python
import jax
import jax.numpy as jnp
from jax import lax
from jax.sharding import Mesh
from jax.sharding import PartitionSpec as P

BINS = 256
GX = ("gx_0", "gx_1")
GZ = ("gz_0", "gz_1")
GX_GY_GZ = ("gx_0", "gx_1", "gy", "gz_0", "gz_1")


stencil_coefficients = (0.8, -0.2, 4.0 / 105.0, -1.0 / 280.0)
grad_range = 12.0


def extended_2(block, sides, width):
    for axis, dim in sides:
        count = lax.axis_size(axis)
        forward = [(i, i + 1) for i in range(count - 1)]
        forward.append((count - 1, 0))
        backward = [(target, source) for source, target in forward]
        low = lax.ppermute(
            lax.slice_in_dim(block, block.shape[dim] - width, None, axis=dim), axis, forward
        )
        high = lax.ppermute(lax.slice_in_dim(block, 0, width, axis=dim), axis, backward)
        block = jnp.concatenate([low, block, high], axis=dim)
    return block


def gathered_once(x, axis):
    leaves = jax.tree.leaves(x)
    turns = sorted(range(len(leaves)), key=lambda k: -leaves[k].size)
    width = (1, *leaves[turns[0]].shape)[-1]
    lines = [
        jnp.pad(leaves[k].reshape(-1), (0, -leaves[k].size % width)).reshape(-1, width)
        for k in turns
    ]
    both, at, found = (lax.all_gather(jnp.concatenate(lines), axis), 0, {})
    for k, line in zip(turns, lines):
        piece = both[:, at : at + len(line)].reshape(len(both), -1)
        found[k] = piece[:, : leaves[k].size].reshape(-1, *leaves[k].shape)
        at += len(line)
    numbers = iter(range(len(leaves)))
    return jax.tree.map(lambda _: found[next(numbers)], x)


def merged_by_axis(x, axes, combine):
    for axis in axes:
        pieces = gathered_once(x, axis)
        x = jax.tree.map(lambda part: part[0], pieces)
        for k in range(1, lax.axis_size(axis)):
            x = combine(x, jax.tree.map(lambda part: part[k], pieces))
    return x


def directional_rate(extended, direction_length_count):
    length = extended.shape[direction_length_count] - 8
    running = jnp.zeros(
        extended.shape[:direction_length_count]
        + (length,)
        + extended.shape[direction_length_count + 1 :],
        jnp.float32,
    )
    for offset, coefficient in enumerate(stencil_coefficients, start=1):
        forward_cells = lax.slice_in_dim(
            extended, 4 + offset, 4 + offset + length, axis=direction_length_count
        )
        backward_cells = lax.slice_in_dim(
            extended, 4 - offset, 4 - offset + length, axis=direction_length_count
        )
        running = running + coefficient * (forward_cells - backward_cells)
    return running


def local_counts(low_bin, fraction):
    cell_count = low_bin.shape[0]
    span_cells = min(cell_count, 32768)
    turn_count = cell_count // span_cells
    coarse_rows = BINS // 16
    coarse_ids = jnp.arange(coarse_rows, dtype=jnp.int32)[:, None]
    finer_ids = jnp.arange(16, dtype=jnp.int32)[:, None]

    def one_turn(turn_index, running):
        start = turn_index * span_cells
        low_part = lax.dynamic_slice_in_dim(low_bin, start, span_cells)
        frac_part = lax.dynamic_slice_in_dim(fraction, start, span_cells)
        high_part = low_part + 1
        coarse = jnp.concatenate([low_part // 16, high_part // 16])
        finer = jnp.concatenate([low_part % 16, high_part % 16])
        weight = jnp.concatenate([1.0 - frac_part, frac_part])
        left_side = jnp.where(coarse[None, :] == coarse_ids, weight[None, :], 0.0)
        right_side = (finer[None, :] == finer_ids).astype(jnp.float32)
        product = lax.dot_general(
            left_side,
            right_side,
            (((1,), (1,)), ((), ())),
            precision=lax.Precision.HIGHEST,
            preferred_element_type=jnp.float32,
        )
        return running + product

    running = lax.fori_loop(0, turn_count, one_turn, jnp.zeros((coarse_rows, 16), jnp.float32))
    return running.reshape(BINS)


def combine_all(first, second):
    return (
        first[0] + second[0],
        first[1] + second[1],
        first[2] + second[2],
        jnp.maximum(first[3], second[3]),
        jnp.minimum(first[4], second[4]),
    )


def on_device(heat_level_grid, interval_first_class, interval_beyond_class):
    grad_x = directional_rate(extended_2(heat_level_grid, ((GX, 2),), 4), 2)
    grad_y = directional_rate(extended_2(heat_level_grid, (("gy", 1),), 4), 1)
    grad_z = directional_rate(extended_2(heat_level_grid, ((GZ, 0),), 4), 0)
    slope_norm_square = grad_z * grad_z + grad_y * grad_y + grad_x * grad_x
    magnitude = jnp.sqrt(slope_norm_square + 1.0) - 1.0
    position = jnp.clip(magnitude * (BINS / grad_range), 0.5, BINS - 0.5)
    low_bin = jnp.minimum(jnp.floor(position - 0.5), BINS - 2).astype(jnp.int32)
    fraction = position - 0.5 - low_bin.astype(jnp.float32)
    counts = local_counts(low_bin.reshape(-1), fraction.reshape(-1))
    lower_edge = interval_first_class[0]
    upper_edge = interval_beyond_class[0]
    high_bin = low_bin + 1
    inside_low = (low_bin >= lower_edge) & (low_bin < upper_edge)
    inside_high = (high_bin >= lower_edge) & (high_bin < upper_edge)
    weight = jnp.where(inside_low, 1.0 - fraction, 0.0) + jnp.where(inside_high, fraction, 0.0)
    lowest = jnp.min(magnitude + grad_range * (1.0 - weight))
    highest = jnp.max(weight * magnitude)
    weighted_sum = jnp.sum(weight * magnitude)
    weighted_count = jnp.sum(weight)
    counts, weighted_sum, weighted_count, highest, lowest = merged_by_axis(
        (counts, weighted_sum, weighted_count, highest, lowest), GX_GY_GZ, combine_all
    )
    total_cells = (
        heat_level_grid.shape[0]
        * heat_level_grid.shape[1]
        * heat_level_grid.shape[2]
        * lax.axis_size(GX)
        * lax.axis_size("gy")
        * lax.axis_size(GZ)
    )
    histogram = counts * (BINS / total_cells)
    stats = jnp.stack([lowest, highest, weighted_sum / total_cells, weighted_count / total_cells])
    return (magnitude, histogram, stats)


def solution(mesh):
    finer = Mesh(
        mesh.devices.reshape(2, 2, mesh.shape["gy"], 2, 4), ("gx_0", "gx_1", "gy", "gz_0", "gz_1")
    )
    return jax.shard_map(
        on_device,
        mesh=finer,
        in_specs=(P(GZ, "gy", GX), P(), P()),
        out_specs=(P(GZ, "gy", GX), P(), P()),
        check_vma=False,
    )
```

profile of v0, /device:TPU:24, one launch (start us, length us, event | category | flops | bytes accessed | tf_op | source)
XLA Modules:
  0.0 224.6 jit_solution(5636302203498421307)
XLA Ops:
  0.6 1.6 fusion.69
  2.3 3.4 %collective-permute-start.1 = (f32[4,64,128]{2,1,0:T(8,128)}, f32[4,64,128]{2,1,0:T(8,128)S(1)}, u32[]{:S(2)}, u32[]{:S(2)}) collective-permute-start(f32[4,64,128]{2,1,0:T(8,128)} %get-tuple-element.248), channel_id=1, source_target_pairs={{0,1},{1,2},{2,3},{3,4},{4,5},{5,6},{6,7},{7,0},{8,9},{9,10},{10,1... | collective-permute-start | bytes 393224 | tf_op jit(solution)/shard_map/ppermute | solution.py:23
  5.7 4.6 %collective-permute-start = (f32[4,64,128]{2,1,0:T(8,128)S(1)}, f32[4,64,128]{2,1,0:T(8,128)S(1)}, u32[]{:S(2)}, u32[]{:S(2)}) collective-permute-start(f32[4,64,128]{2,1,0:T(8,128)S(1)} %get-tuple-element.247), channel_id=1, source_target_pairs={{1,0},{2,1},{3,2},{4,3},{5,4},{6,5},{7,6},{0,7},{9,8},{10,9},{11,1... | collective-permute-start | bytes 393224 | tf_op jit(solution)/shard_map/ppermute | solution.py:26
  10.2 1.9 fusion.71
  13.2 1.9 collective-permute-start.5
  15.5 5.1 %collective-permute-start.4 = (f32[32,64,4]{1,0,2:T(8,128)S(1)}, f32[32,64,4]{1,0,2:T(8,128)}, u32[]{:S(2)}, u32[]{:S(2)}) collective-permute-start(f32[32,64,4]{1,0,2:T(8,128)S(1)} %copy.31), channel_id=1, source_target_pairs={{128,0},{256,128},{384,256},{0,384},{129,1},{257,129},{385,257},{1... | collective-permute-start | bytes 98312 | tf_op jit(solution)/shard_map/ppermute | solution.py:26
  21.3 11.4 %collective-permute-start.2 = (f32[32,4,128]{2,1,0:T(4,128)}, f32[32,4,128]{2,1,0:T(4,128)}, u32[]{:S(2)}, u32[]{:S(2)}) collective-permute-start(f32[32,4,128]{2,1,0:T(4,128)} %get-tuple-element.252), channel_id=1, source_target_pairs={{8,0},{16,8},{24,16},{32,24},{40,32},{48,40},{56,48},{64,56},{72,6... | collective-permute-start | bytes 196616 | tf_op jit(solution)/shard_map/ppermute | solution.py:26
  34.0 1.9 collective-permute-start.3
  38.9 2.8 %collective-permute-done.3 = f32[32,4,128]{2,1,0:T(4,128)} collective-permute-done((f32[32,4,128]{2,1,0:T(4,128)}, f32[32,4,128]{2,1,0:T(4,128)}, u32[]{:S(2)}, u32[]{:S(2)}) %collective-permute-start.3) | collective-permute-done | bytes 65568 | tf_op jit(solution)/shard_map/ppermute | solution.py:23
  41.7 6.2 %add_reduce_fusion = (f32[]{:T(128)}, f32[]{:T(128)}, f32[]{:T(128)}, f32[]{:T(128)}, f32[32,64,128]{2,1,0:T(8,128)S(1)}) fusion(s32[]{:T(128)} %bitcast.122, s32[]{:T(128)} %bitcast.121, f32[32,64,128]{2,1,0:T(8,128)S(1)} %copy-done, f32[32,64,4]{2,1,0:T(8,128)S(1)} %copy.10, f32[32,64,4]{2,1,0:T(8,128)S(1)} %copy.8, ...), kind=kLoop, calls=%fused_computation.103 | loop fusion | flops 20709376 | bytes 14811160 | tf_op jit(solution)/shard_map/reduce_min | solution.py:133
  49.3 43.6 %while.18 = (s32[]{:T(128)}, f32[16,16]{1,0:T(8,128)S(1)}, s32[262144]{0:T(1024)S(1)}, f32[262144]{0:T(1024)}, s32[]{:T(128)}, /*index=5*/s32[]{:T(128)}, s32[]{:T(128)}, s32[]{:T(128)}) while((s32[]{:T(128)}, f32[16,16]{1,0:T(8,128)S(1)}, s32[262144]{0:T(1024)S(1)}, f32[262144]{0:T(1024)}, s32[]{:T(128)}, ...), condition=%wide.region_1.2_spmd.clone.clone, body=%wide.region_0.1_spmd.clone.clone.sunk | while | flops 206176768 | bytes 5703833 | solution.py:103
  51.2 3.6 %fusion.106 = f32[16,16]{1,0:T(8,128)S(1)} fusion(f32[65536]{0:T(1024)S(1)} %pad_maximum_fusion.6, s32[65536]{0:T(1024)S(1)} %get-tuple-element.425, f32[16,16]{1,0:T(8,128)S(1)} %get-tuple-element.436, pred[]{:T(512)S(6)} %compare.49, pred[16,65536]{1,0:T(8,128)(4,1)S(1)} %iota_compare_fusion.11), kind=kOutput, calls=%fused_computation.9.clone.3 | convolution fusion | flops 203424256 | bytes 1574913 | tf_op jit(solution)/shard_map/while/body/eval_jaxpr/dot_general | solution.py:94
  56.6 3.6 %fusion.106 = f32[16,16]{1,0:T(8,128)S(1)} fusion(f32[65536]{0:T(1024)S(1)} %pad_maximum_fusion.6, s32[65536]{0:T(1024)S(1)} %get-tuple-element.425, f32[16,16]{1,0:T(8,128)S(1)} %get-tuple-element.436, pred[]{:T(512)S(6)} %compare.49, pred[16,65536]{1,0:T(8,128)(4,1)S(1)} %iota_compare_fusion.11), kind=kOutput, calls=%fused_computation.9.clone.3 | convolution fusion | flops 203424256 | bytes 1574913 | tf_op jit(solution)/shard_map/while/body/eval_jaxpr/dot_general | solution.py:94
  62.1 3.6 %fusion.106 = f32[16,16]{1,0:T(8,128)S(1)} fusion(f32[65536]{0:T(1024)S(1)} %pad_maximum_fusion.6, s32[65536]{0:T(1024)S(1)} %get-tuple-element.425, f32[16,16]{1,0:T(8,128)S(1)} %get-tuple-element.436, pred[]{:T(512)S(6)} %compare.49, pred[16,65536]{1,0:T(8,128)(4,1)S(1)} %iota_compare_fusion.11), kind=kOutput, calls=%fused_computation.9.clone.3 | convolution fusion | flops 203424256 | bytes 1574913 | tf_op jit(solution)/shard_map/while/body/eval_jaxpr/dot_general | solution.py:94
  67.5 3.6 %fusion.106 = f32[16,16]{1,0:T(8,128)S(1)} fusion(f32[65536]{0:T(1024)S(1)} %pad_maximum_fusion.6, s32[65536]{0:T(1024)S(1)} %get-tuple-element.425, f32[16,16]{1,0:T(8,128)S(1)} %get-tuple-element.436, pred[]{:T(512)S(6)} %compare.49, pred[16,65536]{1,0:T(8,128)(4,1)S(1)} %iota_compare_fusion.11), kind=kOutput, calls=%fused_computation.9.clone.3 | convolution fusion | flops 203424256 | bytes 1574913 | tf_op jit(solution)/shard_map/while/body/eval_jaxpr/dot_general | solution.py:94
  73.0 3.6 %fusion.106 = f32[16,16]{1,0:T(8,128)S(1)} fusion(f32[65536]{0:T(1024)S(1)} %pad_maximum_fusion.6, s32[65536]{0:T(1024)S(1)} %get-tuple-element.425, f32[16,16]{1,0:T(8,128)S(1)} %get-tuple-element.436, pred[]{:T(512)S(6)} %compare.49, pred[16,65536]{1,0:T(8,128)(4,1)S(1)} %iota_compare_fusion.11), kind=kOutput, calls=%fused_computation.9.clone.3 | convolution fusion | flops 203424256 | bytes 1574913 | tf_op jit(solution)/shard_map/while/body/eval_jaxpr/dot_general | solution.py:94
  78.4 3.6 %fusion.106 = f32[16,16]{1,0:T(8,128)S(1)} fusion(f32[65536]{0:T(1024)S(1)} %pad_maximum_fusion.6, s32[65536]{0:T(1024)S(1)} %get-tuple-element.425, f32[16,16]{1,0:T(8,128)S(1)} %get-tuple-element.436, pred[]{:T(512)S(6)} %compare.49, pred[16,65536]{1,0:T(8,128)(4,1)S(1)} %iota_compare_fusion.11), kind=kOutput, calls=%fused_computation.9.clone.3 | convolution fusion | flops 203424256 | bytes 1574913 | tf_op jit(solution)/shard_map/while/body/eval_jaxpr/dot_general | solution.py:94
  83.9 3.6 %fusion.106 = f32[16,16]{1,0:T(8,128)S(1)} fusion(f32[65536]{0:T(1024)S(1)} %pad_maximum_fusion.6, s32[65536]{0:T(1024)S(1)} %get-tuple-element.425, f32[16,16]{1,0:T(8,128)S(1)} %get-tuple-element.436, pred[]{:T(512)S(6)} %compare.49, pred[16,65536]{1,0:T(8,128)(4,1)S(1)} %iota_compare_fusion.11), kind=kOutput, calls=%fused_computation.9.clone.3 | convolution fusion | flops 203424256 | bytes 1574913 | tf_op jit(solution)/shard_map/while/body/eval_jaxpr/dot_general | solution.py:94
  89.3 3.6 %fusion.106 = f32[16,16]{1,0:T(8,128)S(1)} fusion(f32[65536]{0:T(1024)S(1)} %pad_maximum_fusion.6, s32[65536]{0:T(1024)S(1)} %get-tuple-element.425, f32[16,16]{1,0:T(8,128)S(1)} %get-tuple-element.436, pred[]{:T(512)S(6)} %compare.49, pred[16,65536]{1,0:T(8,128)(4,1)S(1)} %iota_compare_fusion.11), kind=kOutput, calls=%fused_computation.9.clone.3 | convolution fusion | flops 203424256 | bytes 1574913 | tf_op jit(solution)/shard_map/while/body/eval_jaxpr/dot_general | solution.py:94
  95.5 5.9 %all-gather.5 = f32[2,5,256]{2,1,0:T(8,128)S(1)} all-gather(f32[1,5,256]{2,1,0:T(8,128)S(1)} %bitcast.128), channel_id=2, replica_groups=mesh['gx_0'=2,'gx_1'=2,'gy'=16,'gz_0'=2,'gz_1'=4] {'gx_0'}, dimensions={0}, use_global_device_ids=true | all-gather | bytes 15360 | tf_op jit(solution)/shard_map/all_gather | solution.py:39
  108.8 1.8 all-gather.6
  118.0 27.0 %all-gather.7 = f32[16,5,256]{2,1,0:T(8,128)S(1)} all-gather(f32[1,5,256]{2,1,0:T(8,128)S(1)} %bitcast.130), channel_id=4, replica_groups=mesh['gx_0'=2,'gx_1'=2,'gy'=16,'gz_0'=2,'gz_1'=4] {'gy'}, dimensions={0}, use_global_device_ids=true | all-gather | bytes 87040 | tf_op jit(solution)/shard_map/all_gather | solution.py:39
  187.5 4.4 %all-gather.8 = f32[2,5,256]{2,1,0:T(8,128)S(1)} all-gather(f32[1,5,256]{2,1,0:T(8,128)S(1)} %bitcast.131), channel_id=5, replica_groups=mesh['gx_0'=2,'gx_1'=2,'gy'=16,'gz_0'=2,'gz_1'=4] {'gz_0'}, dimensions={0}, use_global_device_ids=true | all-gather | bytes 15360 | tf_op jit(solution)/shard_map/all_gather | solution.py:39
  199.3 11.9 %all-gather.9 = f32[4,5,256]{2,1,0:T(8,128)S(1)} all-gather(f32[1,5,256]{2,1,0:T(8,128)S(1)} %bitcast.132), channel_id=6, replica_groups=mesh['gx_0'=2,'gx_1'=2,'gy'=16,'gz_0'=2,'gz_1'=4] {'gz_1'}, dimensions={0}, use_global_device_ids=true | all-gather | bytes 25600 | tf_op jit(solution)/shard_map/all_gather | solution.py:39
  (143 shorter events, 36.1 us)
Async XLA Ops:
  2.3 35.3 %collective-permute-start.1 = (f32[4,64,128]{2,1,0:T(8,128)}, f32[4,64,128]{2,1,0:T(8,128)S(1)}, u32[]{:S(2)}, u32[]{:S(2)}) collective-permute-start(f32[4,64,128]{2,1,0:T(8,128)} %get-tuple-element.248), channel_id=1, source_target_pairs={{0,1},{1,2},{2,3},{3,4},{4,5},{5,6},{6,7},{7,0},{8,9},{9,10},{10,1... | collective-permute-start | bytes 393224 | tf_op jit(solution)/shard_map/ppermute | solution.py:23
  5.7 32.3 %collective-permute-start = (f32[4,64,128]{2,1,0:T(8,128)S(1)}, f32[4,64,128]{2,1,0:T(8,128)S(1)}, u32[]{:S(2)}, u32[]{:S(2)}) collective-permute-start(f32[4,64,128]{2,1,0:T(8,128)S(1)} %get-tuple-element.247), channel_id=1, source_target_pairs={{1,0},{2,1},{3,2},{4,3},{5,4},{6,5},{7,6},{0,7},{9,8},{10,9},{11,1... | collective-permute-start | bytes 393224 | tf_op jit(solution)/shard_map/ppermute | solution.py:26
  12.2 8.5 %copy-start = (f32[32,64,128]{2,1,0:T(8,128)S(1)}, f32[32,64,128]{2,1,0:T(8,128)}, u32[]{:S(2)}) copy-start(f32[32,64,128]{2,1,0:T(8,128)} %param.5) | copy-start | bytes 3145732
  13.2 20.8 %collective-permute-start.5 = (f32[32,64,4]{1,0,2:T(8,128)}, f32[32,64,4]{1,0,2:T(8,128)S(1)}, u32[]{:S(2)}, u32[]{:S(2)}) collective-permute-start(f32[32,64,4]{1,0,2:T(8,128)} %copy.32), channel_id=1, source_target_pairs={{0,128},{128,256},{256,384},{384,0},{1,129},{129,257},{257,385},{3... | collective-permute-start | bytes 98312 | tf_op jit(solution)/shard_map/ppermute | solution.py:23
  15.5 20.9 %collective-permute-start.4 = (f32[32,64,4]{1,0,2:T(8,128)S(1)}, f32[32,64,4]{1,0,2:T(8,128)}, u32[]{:S(2)}, u32[]{:S(2)}) collective-permute-start(f32[32,64,4]{1,0,2:T(8,128)S(1)} %copy.31), channel_id=1, source_target_pairs={{128,0},{256,128},{384,256},{0,384},{129,1},{257,129},{385,257},{1... | collective-permute-start | bytes 98312 | tf_op jit(solution)/shard_map/ppermute | solution.py:26
  21.3 16.7 %collective-permute-start.2 = (f32[32,4,128]{2,1,0:T(4,128)}, f32[32,4,128]{2,1,0:T(4,128)}, u32[]{:S(2)}, u32[]{:S(2)}) collective-permute-start(f32[32,4,128]{2,1,0:T(4,128)} %get-tuple-element.252), channel_id=1, source_target_pairs={{8,0},{16,8},{24,16},{32,24},{40,32},{48,40},{56,48},{64,56},{72,6... | collective-permute-start | bytes 196616 | tf_op jit(solution)/shard_map/ppermute | solution.py:26
  34.0 7.7 %collective-permute-start.3 = (f32[32,4,128]{2,1,0:T(4,128)}, f32[32,4,128]{2,1,0:T(4,128)}, u32[]{:S(2)}, u32[]{:S(2)}) collective-permute-start(f32[32,4,128]{2,1,0:T(4,128)} %get-tuple-element.253), channel_id=1, source_target_pairs={{0,8},{8,16},{16,24},{24,32},{32,40},{40,48},{48,56},{56,64},{64,7... | collective-permute-start | bytes 196616 | tf_op jit(solution)/shard_map/ppermute | solution.py:23
  47.9 1.4 copy-start.1
where the time goes:
time: 226 us; the launch traced here: 225 us
  between operations  67.5 us (30%)
  blocking collectives  51 us (23%)
  matrix products  28.5 us (13%)
  starting transfers between devices  28.3 us (13%)
  other arithmetic  23.3 us (10%)
  local copies, waits for them, and re-layouts  22.6 us (10%)
  waiting for transfers between devices  2.81 us (1%)
    all_gather x5, blocking collectives, gathered_once(): both, at, found = (lax.all_gather(jnp.concatenate(lines), axis), 0, {})  51 us
    dot_general x8, matrix products, one_turn(): lax.dot_general(left_side, right_side, (((1,), (1,)), ((), ())), precisio...  28.5 us
    ppermute x3, starting transfers between devices, extended_2(): lax.ppermute(lax.slice_in_dim(block, 0, width, axis=dim), axis, backward)  21.1 us
    slice x20, local copies, waits for them, and re-layouts, merged_by_axis(): x = combine(x, jax.tree.map(lambda part: part[k], pieces))  11.2 us
    sub x8, other arithmetic, one_turn(): weight = jnp.concatenate([1.0 - frac_part, frac_part])  7.43 us
    ppermute x3, starting transfers between devices, extended_2(): lax.ppermute(lax.slice_in_dim(block, block.shape[dim] - width, None, axis...  7.22 us
    reduce_min x1, other arithmetic, on_device(): lowest = jnp.min(magnitude + grad_range * (1.0 - weight))  6.22 us
  transfers between devices with their start and end apart: 6, of which 1 were waited for; matrix products, arithmetic and copies ran while one was open for 3% of the time, Pallas kernels for 0%

commit v1 on v0

v1 whole, which is shorter than its diff:
```python
import functools

import jax
import jax.numpy as jnp
from jax import lax
from jax.experimental import pallas as pl
from jax.experimental.pallas import tpu as pltpu
from jax.sharding import PartitionSpec as P

MESH = pl.DeviceIdType.MESH
BINS = 256
RANGE = 12.0
COEF = (0.8, -0.2, 4.0 / 105.0, -1.0 / 280.0)


def kernel(
    sizes, cells, edges, u_hbm, mag_ref, hist_ref, stat_ref,
    ext, packed, from_low, from_high, acc, msg, plane, line,
    in_sem, send_sem, recv_sem, plane_send, plane_recv, line_send, line_recv,
):
    nx, ny, nz = sizes
    dz, dy, dx = u_hbm.shape
    tiles = dy // 8
    gx, gy, gz = lax.axis_index("gx"), lax.axis_index("gy"), lax.axis_index("gz")

    def device(a=0, c=0, b=0):
        return {
            "gx": lax.rem(gx + (a + nx), nx),
            "gy": lax.rem(gy + (c + ny), ny),
            "gz": lax.rem(gz + (b + nz), nz),
        }

    plane_peers = [(a, b) for a in range(nx) for b in range(nz)][1:]

    own = ext.at[pl.ds(4, dz), pl.ds(8, dy), :]
    load = pltpu.make_async_copy(u_hbm, own, in_sem)
    load.start()
    barrier = pltpu.get_barrier_semaphore()
    for a, b in plane_peers:
        pl.semaphore_signal(barrier, inc=1, device_id=device(a=a, b=b), device_id_type=MESH)
    for c in range(1, ny):
        pl.semaphore_signal(barrier, inc=1, device_id=device(c=c), device_id_type=MESH)
    load.wait()

    lane = lax.broadcasted_iota(jnp.int32, (8, dx), 1)

    def pack(p, _):
        out = jnp.zeros((8, dx), jnp.float32)
        for j in range(16):
            cell = ext[4 + 2 * p + j // 8, pl.ds(8 + 8 * (j % 8), 8), :]
            moved = pltpu.roll(cell, 8 * j + 4, 1)
            out = jnp.where(lane // 8 == j, moved, out)
        packed[p] = out
        return 0

    lax.fori_loop(0, dz // 2, pack, 0)

    pl.semaphore_wait(barrier, len(plane_peers) + ny - 1)

    def send(k, src, dst, **offset):
        copy = pltpu.make_async_remote_copy(
            src_ref=src, dst_ref=dst, send_sem=send_sem.at[k], recv_sem=recv_sem.at[k],
            device_id=device(**offset), device_id_type=MESH,
        )
        copy.start()
        return copy

    rows = pl.ds(8, dy)
    planes = pl.ds(4, dz)
    copies = [
        send(0, ext.at[planes, pl.ds(8, 4), :], ext.at[planes, pl.ds(8 + dy, 4), :], c=-1),
        send(1, ext.at[planes, pl.ds(4 + dy, 4), :], ext.at[planes, pl.ds(4, 4), :], c=1),
        send(2, packed, from_high, a=-1),
        send(3, packed, from_low, a=1),
        send(4, ext.at[pl.ds(4, 4), rows, :], ext.at[pl.ds(4 + dz, 4), rows, :], b=-1),
        send(5, ext.at[pl.ds(dz, 4), rows, :], ext.at[pl.ds(0, 4), rows, :], b=1),
    ]
    acc[...] = jnp.zeros_like(acc)
    for copy in copies:
        copy.wait_send()
        copy.wait_recv()

    low_edge = edges[0].astype(jnp.float32) - 1.0
    high_edge = edges[1].astype(jnp.float32) - 1.0
    half = lax.broadcasted_iota(jnp.int32, (16, dx), 0) // 8
    half = half.astype(jnp.float32)

    def pair(x):
        return jnp.concatenate([x, x], axis=0)

    def one_slab(p, carry):
        wsum, wmax, wmin = carry
        rims = jnp.where(lane % 8 < 4, from_low[p], from_high[p])
        lefts, rights = [], []
        for j in range(16):
            z, y = 4 + 2 * p + j // 8, 8 + 8 * (j % 8)
            center = ext[z, pl.ds(y, 8), :]
            rim = pltpu.roll(rims, (dx - 8 * j - 4) % dx, 1)
            grad_x = grad_y = grad_z = None
            for k, coef in enumerate(COEF, start=1):
                ahead = pltpu.roll(jnp.where(lane < k, rim, center), dx - k, 1)
                behind = pltpu.roll(jnp.where(lane >= dx - k, rim, center), k, 1)
                term_x = coef * (ahead - behind)
                term_y = coef * (ext[z, pl.ds(y + k, 8), :] - ext[z, pl.ds(y - k, 8), :])
                term_z = coef * (ext[z + k, pl.ds(y, 8), :] - ext[z - k, pl.ds(y, 8), :])
                grad_x = term_x if grad_x is None else grad_x + term_x
                grad_y = term_y if grad_y is None else grad_y + term_y
                grad_z = term_z if grad_z is None else grad_z + term_z
            square = grad_z * grad_z + grad_y * grad_y + grad_x * grad_x
            magnitude = jnp.sqrt(square + 1.0) - 1.0
            mag_ref[2 * p + j // 8, pl.ds(8 * (j % 8), 8), :] = magnitude
            place = jnp.clip(magnitude * (BINS / RANGE) - 0.5, 0.0, BINS - 1.0)
            low = jnp.minimum(jnp.floor(place), BINS - 2.0)
            fraction = place - low
            weight = jnp.clip(place - low_edge, 0.0, 1.0) - jnp.clip(place - high_edge, 0.0, 1.0)
            value = weight * magnitude
            wsum = wsum + value
            wmax = jnp.maximum(wmax, value)
            wmin = jnp.minimum(wmin, (magnitude + RANGE) - RANGE * weight)
            coarse = jnp.floor(low * 0.125)
            fine = low - 8.0 * coarse
            coarse = (pair(coarse) - half).astype(jnp.bfloat16)
            fine = (pair(fine) - half).astype(jnp.bfloat16)
            part = fraction.astype(jnp.bfloat16)
            rest = (fraction - part.astype(jnp.float32)).astype(jnp.bfloat16)
            part, rest = pair(part), pair(rest)
            one = jnp.ones((16, dx), jnp.bfloat16)
            zero = jnp.zeros((16, dx), jnp.bfloat16)
            lefts.append(
                jnp.concatenate(
                    [jnp.where(coarse == jnp.bfloat16(2 * k), one, zero) for k in range(16)], axis=0
                )
            )
            hits = [fine == jnp.bfloat16(2 * k) for k in range(4)]
            rights.append(
                jnp.concatenate(
                    [jnp.where(hit, term, zero) for term in (one, part, rest) for hit in hits], axis=0
                )
            )
        acc[...] += lax.dot_general(
            jnp.concatenate(lefts, axis=1), jnp.concatenate(rights, axis=1),
            (((1,), (1,)), ((), ())), preferred_element_type=jnp.float32,
        )
        return wsum, wmax, wmin

    nothing = jnp.zeros((8, dx), jnp.float32)
    wsum, wmax, wmin = lax.fori_loop(
        0, dz // 2, one_slab, (nothing, nothing, jnp.full((8, dx), 1e30, jnp.float32))
    )

    total = acc[...]
    same = (
        lax.broadcasted_iota(jnp.int32, total.shape, 0) % 8
        == lax.broadcasted_iota(jnp.int32, total.shape, 1) % 8
    )
    total = jnp.where(same, total, 0.0).reshape(32, 8, 192).sum(axis=1)
    source = lax.broadcasted_iota(jnp.int32, (192, 128), 0)
    target = lax.broadcasted_iota(jnp.int32, (192, 128), 1)
    fits = (source // 8) % 8 == target % 8
    coarse_row = lax.broadcasted_iota(jnp.int32, (32, 128), 0)
    coarse_lane = lax.broadcasted_iota(jnp.int32, (32, 128), 1)
    keep = coarse_row % 16 == coarse_lane // 8

    def bins_of(chosen):
        spread = lax.dot_general(
            total, jnp.where(fits & chosen, 1.0, 0.0), (((1,), (0,)), ((), ())),
            precision=lax.Precision.HIGHEST, preferred_element_type=jnp.float32,
        )
        spread = jnp.where(keep, spread, 0.0)
        return spread[:16].sum(axis=0, keepdims=True), spread[16:].sum(axis=0, keepdims=True)

    number = bins_of(source < 64)
    part = bins_of(source >= 64)
    lane1 = lane[:1]
    turned = [pltpu.roll(pair(pair(pair(x))), 1, 1)[:1] for x in part]
    first = number[0] - part[0] + jnp.where(lane1 == 0, turned[1], turned[0])
    second = number[1] - part[1] + jnp.where(lane1 == 0, turned[0], turned[1])
    third = jnp.where(
        lane1 == 0, jnp.sum(wsum),
        jnp.where(lane1 == 1, jnp.max(wmax), jnp.min(wmin)),
    )
    msg[0:3, :] = jnp.concatenate([first, second, third], axis=0)

    def merged(slots, slot_ref):
        value = slot_ref[0]
        added, most, least = value, value, value
        for k in range(1, slots):
            value = slot_ref[k]
            added, most, least = added + value, jnp.maximum(most, value), jnp.minimum(least, value)
        lane3 = lax.broadcasted_iota(jnp.int32, added.shape, 1)
        row3 = lax.broadcasted_iota(jnp.int32, added.shape, 0)
        return jnp.where(
            (row3 < 2) | (lane3 == 0), added, jnp.where(lane3 == 1, most, least)
        )

    def exchange(peers, slot_ref, send_one, recv_one):
        slots = len(peers) + 1
        slot_ref[0] = msg[...]
        for k, offset in enumerate(peers, start=1):
            pltpu.make_async_remote_copy(
                src_ref=msg, dst_ref=slot_ref.at[k], send_sem=send_one, recv_sem=recv_one,
                device_id=device(**offset), device_id_type=MESH,
            ).start()
        rest = slot_ref.at[pl.ds(1, slots - 1)]
        pltpu.make_async_copy(rest, rest, send_one).wait()
        pltpu.make_async_copy(rest, rest, recv_one).wait()
        return merged(slots, slot_ref)

    msg[...] = exchange([dict(a=a, b=b) for a, b in plane_peers], plane, plane_send, plane_recv)
    done = exchange([dict(c=c) for c in range(1, ny)], line, line_send, line_recv)

    hist_ref[...] = done[0:2] * (BINS / cells)
    bin_id = lax.broadcasted_iota(jnp.int32, (2, 128), 0) * 128 + lax.broadcasted_iota(
        jnp.int32, (2, 128), 1
    )
    inside = (bin_id >= edges[0]) & (bin_id < edges[1])
    number = jnp.sum(jnp.where(inside, done[0:2], 0.0))
    last = done[2:3]
    total, most, least = (
        jnp.sum(jnp.where(lane1 == k, last, 0.0)) for k in range(3)
    )
    stat_ref[...] = jnp.where(
        lane1 == 0, least,
        jnp.where(lane1 == 1, most, jnp.where(lane1 == 2, total, number) * (1.0 / cells)),
    )


def solution(mesh):
    sizes = tuple(mesh.shape[name] for name in ("gx", "gy", "gz"))
    nx, ny, nz = sizes

    def on_device(u, first, beyond):
        dz, dy, dx = u.shape
        cells = u.size * nx * ny * nz
        edges = jnp.concatenate([first, beyond])
        magnitude, hist, stat = pl.pallas_call(
            functools.partial(kernel, sizes, cells),
            out_shape=(
                jax.ShapeDtypeStruct(u.shape, jnp.float32),
                jax.ShapeDtypeStruct((2, 128), jnp.float32),
                jax.ShapeDtypeStruct((1, 128), jnp.float32),
            ),
            in_specs=[
                pl.BlockSpec(memory_space=pltpu.SMEM),
                pl.BlockSpec(memory_space=pl.ANY),
            ],
            out_specs=(
                pl.BlockSpec(memory_space=pltpu.VMEM),
                pl.BlockSpec(memory_space=pltpu.VMEM),
                pl.BlockSpec(memory_space=pltpu.VMEM),
            ),
            scratch_shapes=[
                pltpu.VMEM((dz + 8, dy + 16, dx), jnp.float32),
                pltpu.VMEM((dz // 2, 8, dx), jnp.float32),
                pltpu.VMEM((dz // 2, 8, dx), jnp.float32),
                pltpu.VMEM((dz // 2, 8, dx), jnp.float32),
                pltpu.VMEM((256, 192), jnp.float32),
                pltpu.VMEM((3, 128), jnp.float32),
                pltpu.VMEM((nx * nz, 3, 128), jnp.float32),
                pltpu.VMEM((ny, 3, 128), jnp.float32),
                pltpu.SemaphoreType.DMA,
                pltpu.SemaphoreType.DMA((6,)),
                pltpu.SemaphoreType.DMA((6,)),
                pltpu.SemaphoreType.DMA,
                pltpu.SemaphoreType.DMA,
                pltpu.SemaphoreType.DMA,
                pltpu.SemaphoreType.DMA,
            ],
            compiler_params=pltpu.CompilerParams(collective_id=0, has_side_effects=True),
        )(edges, u)
        return magnitude, hist.reshape(BINS), stat[0, :4]

    return jax.shard_map(
        on_device,
        mesh=mesh,
        in_specs=(P("gz", "gy", "gx"), P(), P()),
        out_specs=(P("gz", "gy", "gx"), P(), P()),
        check_vma=False,
    )
```

time: 226 us -> 55.6 us (0.25)
  the two profiles are of different devices: /device:TPU:24 before, /device:TPU:1 now
where the time goes in v1:
time: 55.6 us; the launch traced here: 55.4 us
  Pallas kernels  48.9 us (88%)
  local copies, waits for them, and re-layouts  3.95 us (7%)
  between operations  1.94 us (3%)
  other arithmetic  0.59 us (1%)
    pallas_call x1, Pallas kernels, on_device(): pl.pallas_call(functools.partial(kernel, sizes, cells), out_shape=(jax.Sh...  48.9 us
    unnamed x6, local copies, waits for them, and re-layouts  3.44 us

profile of v1, /device:TPU:1, one launch (start us, length us, event | category | flops | bytes accessed | tf_op | source)
XLA Modules:
  0.0 55.4 jit_solution(11688001703059834349)
XLA Ops:
  1.9 0.6 %pad_add_fusion.edges = s32[2]{0:T(128)} fusion(s32[1]{0:T(128)S(6)} %copy.9, s32[1]{0:T(128)S(6)} %copy.8), kind=kLoop, calls=%fused_computation | loop fusion | flops 2 | bytes 16 | tf_op jit(solution)/shard_map/concatenate | solution.py:235
  2.5 48.9 %shard_map.58 = (f32[32,64,128]{2,1,0:T(8,128)}, f32[2,128]{1,0:T(2,128)}, f32[1,128]{1,0:T(1,128)}) custom-call(s32[2]{0:T(128)} %pad_add_fusion.edges, f32[32,64,128]{2,1,0:T(8,128)} %u_hbm.1), custom_call_target="tpu_custom_call" | custom-call | tf_op jit(solution)/shard_map/pallas_call | solution.py:236
  51.4 0.0 copy-start.1
  51.4 0.6 %copy-done.1 = f32[1,128]{1,0:T(1,128)S(1)} copy-done((f32[1,128]{1,0:T(1,128)S(1)}, f32[1,128]{1,0:T(1,128)}, u32[]{:S(2)}) %copy-start.1) | copy-done | bytes 536
  52.0 0.5 slice_bitcast_fusion
  52.5 0.0 copy-start
  52.5 2.3 %copy.10 = f32[32,64,128]{2,1,0:T(8,128)} copy(f32[32,64,128]{2,1,0:T(8,128)} %get-tuple-element.12) | data formatting | bytes 2097152
  54.8 0.0 copy-done
  54.8 0.6 %copy.11 = f32[256]{0:T(256)} copy(f32[256]{0:T(256)S(1)} %bitcast.3) | data formatting | bytes 2048
Async XLA Ops:
  51.4 0.6 %copy-start.1 = (f32[1,128]{1,0:T(1,128)S(1)}, f32[1,128]{1,0:T(1,128)}, u32[]{:S(2)}) copy-start(f32[1,128]{1,0:T(1,128)} %get-tuple-element.8) | copy-start | bytes 1540
  52.5 2.3 %copy-start = (f32[2,128]{1,0:T(2,128)S(1)}, f32[2,128]{1,0:T(2,128)}, u32[]{:S(2)}) copy-start(f32[2,128]{1,0:T(2,128)} %get-tuple-element.7) | copy-start | bytes 3076

commit v2 on v1

v2 whole, which is shorter than its diff:
```python
import functools

import jax
import jax.numpy as jnp
from jax import lax
from jax.experimental import pallas as pl
from jax.experimental.pallas import tpu as pltpu
from jax.sharding import PartitionSpec as P

MESH = pl.DeviceIdType.MESH
BINS = 256
RANGE = 12.0
COEF = (0.8, -0.2, 4.0 / 105.0, -1.0 / 280.0)


def pair(x):
    return jnp.concatenate([x, x], axis=0)


def kernel(
    sizes, cells, u_hbm, first_hbm, beyond_hbm, mag_ref, hist_ref, stat_ref,
    ext, packed, from_low, from_high, rim_x, rim_yz, acc, msg, plane, line, first, beyond,
    in_sem, edge_sem, send_sem, recv_sem, plane_send, plane_recv, line_send, line_recv,
    near2, near3, far2, far3,
):
    nx, ny, nz = sizes
    dz, dy, dx = u_hbm.shape
    gx, gy, gz = lax.axis_index("gx"), lax.axis_index("gy"), lax.axis_index("gz")

    def device(a=0, c=0, b=0):
        return {
            "gx": lax.rem(gx + (a + nx), nx) if a else gx,
            "gy": lax.rem(gy + (c + ny), ny) if c else gy,
            "gz": lax.rem(gz + (b + nz), nz) if b else gz,
        }

    def signal(sem, **offset):
        pl.semaphore_signal(sem, inc=1, device_id=device(**offset), device_id_type=MESH)

    load = pltpu.make_async_copy(u_hbm, ext.at[pl.ds(4, dz), pl.ds(8, dy), :], in_sem)
    load.start()
    barrier = pltpu.get_barrier_semaphore()
    for offset in (dict(a=-1), dict(a=1), dict(c=-1), dict(c=1), dict(b=-1), dict(b=1)):
        signal(barrier, **offset)
    edge_loads = [
        pltpu.make_async_copy(first_hbm, first, edge_sem.at[0]),
        pltpu.make_async_copy(beyond_hbm, beyond, edge_sem.at[1]),
    ]
    for copy in edge_loads:
        copy.start()

    lane = lax.broadcasted_iota(jnp.int32, (8, dx), 1)
    slot = lane // 8
    left_rim = lane % 8 < 4
    lane16 = lax.broadcasted_iota(jnp.int32, (16, dx), 1)
    half = (lax.broadcasted_iota(jnp.int32, (16, dx), 0) // 8).astype(jnp.float32)
    half_core = jnp.where((lane16 < 4) | (lane16 >= dx - 4), 1000.0, half)
    rim_lane = (lane < 4) | (lane >= dx - 4)

    load.wait()

    def pack(i, _):
        for p in (4 * i, 4 * i + 1, 4 * i + 2, 4 * i + 3):
            out = jnp.zeros((8, dx), jnp.float32)
            for j in range(16):
                cell = ext[4 + 2 * p + j // 8, pl.ds(8 + 8 * (j % 8), 8), :]
                out = jnp.where(slot == j, pltpu.roll(cell, 8 * j + 4, 1), out)
            packed[p] = out
        return 0

    lax.fori_loop(0, dz // 8, pack, 0)

    pl.semaphore_wait(barrier, 6)

    def send(k, src, dst, **offset):
        copy = pltpu.make_async_remote_copy(
            src_ref=src, dst_ref=dst, send_sem=send_sem.at[k], recv_sem=recv_sem.at[k],
            device_id=device(**offset), device_id_type=MESH,
        )
        copy.start()
        return copy

    rows = pl.ds(8, dy)
    planes = pl.ds(4, dz)
    y_rims = [
        send(0, ext.at[planes, pl.ds(8, 4), :], ext.at[planes, pl.ds(8 + dy, 4), :], c=-1),
        send(1, ext.at[planes, pl.ds(4 + dy, 4), :], ext.at[planes, pl.ds(4, 4), :], c=1),
    ]
    xz_rims = [
        send(4, ext.at[pl.ds(4, 4), rows, :], ext.at[pl.ds(4 + dz, 4), rows, :], b=-1),
        send(5, ext.at[pl.ds(dz, 4), rows, :], ext.at[pl.ds(0, 4), rows, :], b=1),
        send(2, packed, from_high, a=-1),
        send(3, packed, from_low, a=1),
    ]
    acc[...] = jnp.zeros_like(acc)
    for copy in edge_loads:
        copy.wait()
    low_edge = first[0].astype(jnp.float32) - 1.0
    high_edge = beyond[0].astype(jnp.float32) - 1.0

    def classify(square, halves, stats):
        wsum, wmax, wmin = stats
        magnitude = jnp.sqrt(square + 1.0) - 1.0
        place = jnp.clip(magnitude * (BINS / RANGE) - 0.5, 0.0, BINS - 1.0)
        low = jnp.minimum(jnp.floor(place), BINS - 2.0)
        fraction = place - low
        weight = jnp.clip(place - low_edge, 0.0, 1.0) - jnp.clip(place - high_edge, 0.0, 1.0)
        value = weight * magnitude
        stats = (
            wsum + value,
            jnp.maximum(wmax, value),
            jnp.minimum(wmin, (magnitude + RANGE) - RANGE * weight),
        )
        coarse = jnp.floor(low * 0.125)
        fine = low - 8.0 * coarse
        coarse = (pair(coarse) - halves).astype(jnp.bfloat16)
        fine = (pair(fine) - half).astype(jnp.bfloat16)
        part = fraction.astype(jnp.bfloat16)
        rest = (fraction - part.astype(jnp.float32)).astype(jnp.bfloat16)
        part, rest = pair(part), pair(rest)
        one = jnp.ones((16, dx), jnp.bfloat16)
        zero = jnp.zeros((16, dx), jnp.bfloat16)
        left = jnp.concatenate(
            [jnp.where(coarse == jnp.bfloat16(2 * k), one, zero) for k in range(16)], axis=0
        )
        hits = [fine == jnp.bfloat16(2 * k) for k in range(4)]
        right = jnp.concatenate(
            [jnp.where(hit, term, zero) for term in (one, part, rest) for hit in hits], axis=0
        )
        return magnitude, left, right, stats

    def count(lefts, rights):
        acc[...] += lax.dot_general(
            jnp.concatenate(lefts, axis=1), jnp.concatenate(rights, axis=1),
            (((1,), (1,)), ((), ())), preferred_element_type=jnp.float32,
        )

    def tiles(pairs, stats, fresh):
        lefts, rights = [], []
        for p, which in pairs:
            if fresh:
                out_x = jnp.zeros((8, dx), jnp.float32)
                out_yz = jnp.zeros((8, dx), jnp.float32)
            else:
                out_x, out_yz = rim_x[p], rim_yz[p]
            for j in which:
                z, y = 4 + 2 * p + j // 8, 8 + 8 * (j % 8)
                center = ext[z, pl.ds(y, 8), :]
                grad_x = grad_y = grad_z = None
                for k, coef in enumerate(COEF, start=1):
                    term_x = coef * (pltpu.roll(center, dx - k, 1) - pltpu.roll(center, k, 1))
                    term_y = coef * (ext[z, pl.ds(y + k, 8), :] - ext[z, pl.ds(y - k, 8), :])
                    term_z = coef * (ext[z + k, pl.ds(y, 8), :] - ext[z - k, pl.ds(y, 8), :])
                    grad_x = term_x if grad_x is None else grad_x + term_x
                    grad_y = term_y if grad_y is None else grad_y + term_y
                    grad_z = term_z if grad_z is None else grad_z + term_z
                square_yz = grad_z * grad_z + grad_y * grad_y
                out_x = jnp.where(slot == j, pltpu.roll(grad_x, 8 * j + 4, 1), out_x)
                out_yz = jnp.where(slot == j, pltpu.roll(square_yz, 8 * j + 4, 1), out_yz)
                magnitude, left, right, stats = classify(
                    square_yz + grad_x * grad_x, half_core, stats
                )
                mag_ref[2 * p + j // 8, pl.ds(8 * (j % 8), 8), :] = magnitude
                lefts.append(left)
                rights.append(right)
            rim_x[p] = out_x
            rim_yz[p] = out_yz
        count(lefts, rights)
        return stats

    inner = [j for j in range(16) if 0 < j % 8 < 7]
    outer = [j for j in range(16) if not 0 < j % 8 < 7]
    nothing = jnp.zeros((8, dx), jnp.float32)
    stats = (nothing, nothing, jnp.full((8, dx), 1e30, jnp.float32))

    stats = lax.fori_loop(
        0, (dz - 8) // 4,
        lambda i, s: tiles([(2 + 2 * i, inner), (3 + 2 * i, inner)], s, True), stats,
    )

    for copy in y_rims:
        copy.wait_send()
        copy.wait_recv()
    if ny > 4:
        signal(far2, c=-2)
        signal(far2, c=2)
    stats = lax.fori_loop(
        0, (dz - 8) // 8,
        lambda i, s: tiles([(2 + 4 * i + k, outer) for k in range(4)], s, False), stats,
    )

    for copy in xz_rims:
        copy.wait_send()
        copy.wait_recv()
    if ny > 4:
        pl.semaphore_wait(far2, 2)
        signal(far3, c=-4)
        signal(far3, c=4)
    if nz > 4:
        signal(near2, b=-2)
        signal(near2, b=2)
        signal(near2, a=2)
    stats = lax.fori_loop(
        0, 4,
        lambda i, s: tiles([(i + (dz // 2 - 4) * (i // 2), range(16))], s, True), stats,
    )
    if nz > 4:
        pl.semaphore_wait(near2, 3)
        signal(near3, b=4)

    rim_stats = (nothing, nothing, jnp.full((8, dx), 1e30, jnp.float32))

    def rims(i, rim_stats):
        lefts, rights = [], []
        for p in [8 * i + k for k in range(8)]:
            own = packed[p]
            high = jnp.where(left_rim, 0.0, from_high[p] - own)
            low = jnp.where(left_rim, from_low[p] - own, 0.0)
            fix_high = fix_low = None
            for k, coef in enumerate(COEF, start=1):
                more = coef * pltpu.roll(high, dx - k, 1)
                less = coef * pltpu.roll(low, k, 1)
                fix_high = more if fix_high is None else fix_high + more
                fix_low = less if fix_low is None else fix_low + less
            grad_x = rim_x[p] + jnp.where(left_rim, fix_high, -fix_low)
            magnitude, left, right, rim_stats = classify(
                rim_yz[p] + grad_x * grad_x, half, rim_stats
            )
            rim_x[p] = magnitude
            lefts.append(left)
            rights.append(right)
        count(lefts, rights)
        return rim_stats

    rim_stats = lax.fori_loop(0, dz // 16, rims, rim_stats)

    wsum = rim_stats[0] + jnp.where(rim_lane, 0.0, stats[0])
    wmax = jnp.maximum(rim_stats[1], jnp.where(rim_lane, 0.0, stats[1]))
    wmin = jnp.minimum(rim_stats[2], jnp.where(rim_lane, 1e30, stats[2]))

    total = acc[...]
    same = (
        lax.broadcasted_iota(jnp.int32, total.shape, 0) % 8
        == lax.broadcasted_iota(jnp.int32, total.shape, 1) % 8
    )
    total = jnp.where(same, total, 0.0).reshape(32, 8, 192).sum(axis=1)
    source = lax.broadcasted_iota(jnp.int32, (192, 128), 0)
    target = lax.broadcasted_iota(jnp.int32, (192, 128), 1)
    fits = (source // 8) % 8 == target % 8
    coarse_row = lax.broadcasted_iota(jnp.int32, (32, 128), 0)
    coarse_lane = lax.broadcasted_iota(jnp.int32, (32, 128), 1)
    keep = coarse_row % 16 == coarse_lane // 8

    def bins_of(chosen):
        spread = lax.dot_general(
            total, jnp.where(fits & chosen, 1.0, 0.0), (((1,), (0,)), ((), ())),
            precision=lax.Precision.HIGHEST, preferred_element_type=jnp.float32,
        )
        spread = jnp.where(keep, spread, 0.0)
        return spread[:16].sum(axis=0, keepdims=True), spread[16:].sum(axis=0, keepdims=True)

    number = bins_of(source < 64)
    part = bins_of(source >= 64)
    lane1 = lane[:1]
    turned = [pltpu.roll(pair(pair(pair(x))), 1, 1)[:1] for x in part]
    row0 = number[0] - part[0] + jnp.where(lane1 == 0, turned[1], turned[0])
    row1 = number[1] - part[1] + jnp.where(lane1 == 0, turned[0], turned[1])
    row2 = jnp.where(
        lane1 == 0, jnp.sum(wsum),
        jnp.where(lane1 == 1, jnp.max(wmax), jnp.min(wmin)),
    )
    msg[0:3, :] = jnp.concatenate([row0, row1, row2], axis=0)

    def merged(slots, slot_ref):
        value = slot_ref[0]
        added, most, least = value, value, value
        for k in range(1, slots):
            value = slot_ref[k]
            added, most, least = added + value, jnp.maximum(most, value), jnp.minimum(least, value)
        lane3 = lax.broadcasted_iota(jnp.int32, added.shape, 1)
        row3 = lax.broadcasted_iota(jnp.int32, added.shape, 0)
        return jnp.where(
            (row3 < 2) | (lane3 == 0), added, jnp.where(lane3 == 1, most, least)
        )

    def spread_out(peers, slot_ref, send_one, recv_one):
        slot_ref[0] = msg[...]
        for k, offset in enumerate(peers, start=1):
            pltpu.make_async_remote_copy(
                src_ref=msg, dst_ref=slot_ref.at[k], send_sem=send_one, recv_sem=recv_one,
                device_id=device(**offset), device_id_type=MESH,
            ).start()

    def gathered(slots, slot_ref, send_one, recv_one):
        rest = slot_ref.at[pl.ds(1, slots - 1)]
        pltpu.make_async_copy(rest, rest, send_one).wait()
        pltpu.make_async_copy(rest, rest, recv_one).wait()
        return merged(slots, slot_ref)

    def far(a, n):
        return min(a, n - a)

    plane_peers = sorted(
        [(a, b) for a in range(nx) for b in range(nz) if a or b],
        key=lambda ab: -(far(ab[0], nx) + far(ab[1], nz)),
    )
    line_peers = sorted(range(1, ny), key=lambda c: -far(c, ny))

    if nz > 4:
        pl.semaphore_wait(near3, 1)
    spread_out([dict(a=a, b=b) for a, b in plane_peers], plane, plane_send, plane_recv)

    def unpack(i, _):
        for p in (4 * i, 4 * i + 1, 4 * i + 2, 4 * i + 3):
            rim = rim_x[p]
            for j in range(16):
                at = (2 * p + j // 8, pl.ds(8 * (j % 8), 8))
                moved = pltpu.roll(rim, (dx - 8 * j - 4) % dx, 1)
                mag_ref[at] = jnp.where(rim_lane, moved, mag_ref[at])
        return 0

    lax.fori_loop(0, dz // 8, unpack, 0)

    msg[...] = gathered(nx * nz, plane, plane_send, plane_recv)
    if ny > 4:
        pl.semaphore_wait(far3, 2)
    spread_out([dict(c=c) for c in line_peers], line, line_send, line_recv)
    done = gathered(ny, line, line_send, line_recv)

    hist_ref[pl.ds(0, 128)] = done[0] * (BINS / cells)
    hist_ref[pl.ds(128, 128)] = done[1] * (BINS / cells)
    bin_id = lax.broadcasted_iota(jnp.int32, (2, 128), 0) * 128 + lax.broadcasted_iota(
        jnp.int32, (2, 128), 1
    )
    inside = (bin_id >= first[0]) & (bin_id < beyond[0])
    number = jnp.sum(jnp.where(inside, done[0:2], 0.0))
    last = done[2:3]
    total, most, least = (jnp.sum(jnp.where(lane1 == k, last, 0.0)) for k in range(3))
    stat_ref[0] = least
    stat_ref[1] = most
    stat_ref[2] = total * (1.0 / cells)
    stat_ref[3] = number * (1.0 / cells)


def solution(mesh):
    sizes = tuple(mesh.shape[name] for name in ("gx", "gy", "gz"))
    nx, ny, nz = sizes

    def on_device(u, first, beyond):
        dz, dy, dx = u.shape
        cells = u.size * nx * ny * nz
        rims = pltpu.VMEM((dz // 2, 8, dx), jnp.float32)
        return pl.pallas_call(
            functools.partial(kernel, sizes, cells),
            out_shape=(
                pltpu.VMEM(u.shape, jnp.float32),
                pltpu.VMEM((BINS,), jnp.float32),
                pltpu.SMEM((4,), jnp.float32),
            ),
            in_specs=[pl.BlockSpec(memory_space=pltpu.HBM)] * 3,
            out_specs=(
                pl.BlockSpec(memory_space=pltpu.VMEM),
                pl.BlockSpec(memory_space=pltpu.VMEM),
                pl.BlockSpec(memory_space=pltpu.SMEM),
            ),
            scratch_shapes=[
                pltpu.VMEM((dz + 8, dy + 16, dx), jnp.float32),
                rims, rims, rims, rims, rims,
                pltpu.VMEM((256, 192), jnp.float32),
                pltpu.VMEM((3, 128), jnp.float32),
                pltpu.VMEM((nx * nz, 3, 128), jnp.float32),
                pltpu.VMEM((ny, 3, 128), jnp.float32),
                pltpu.SMEM((1,), jnp.int32),
                pltpu.SMEM((1,), jnp.int32),
                pltpu.SemaphoreType.DMA,
                pltpu.SemaphoreType.DMA((2,)),
                pltpu.SemaphoreType.DMA((6,)),
                pltpu.SemaphoreType.DMA((6,)),
                pltpu.SemaphoreType.DMA,
                pltpu.SemaphoreType.DMA,
                pltpu.SemaphoreType.DMA,
                pltpu.SemaphoreType.DMA,
                pltpu.SemaphoreType.REGULAR,
                pltpu.SemaphoreType.REGULAR,
                pltpu.SemaphoreType.REGULAR,
                pltpu.SemaphoreType.REGULAR,
            ],
            compiler_params=pltpu.CompilerParams(collective_id=0, has_side_effects=True),
        )(u, first, beyond)

    return jax.shard_map(
        on_device,
        mesh=mesh,
        in_specs=(P("gz", "gy", "gx"), P(), P()),
        out_specs=(P("gz", "gy", "gx"), P(), P()),
        check_vma=False,
    )
```

time: 55.6 us -> 40.3 us (0.72)
  Pallas kernels: 48.9 us -> 36.1 us
  local copies, waits for them, and re-layouts: 3.95 us -> 2.05 us
  other arithmetic: 0.59 us -> 0 us
    pallas_call x1, Pallas kernels: 48.9 us -> 36.1 us  [on_device(): pl.pallas_call(functools.partial(kernel, sizes, cells), out_shape=(pltpu....]
    unnamed x6 -> x3, local copies, waits for them, and re-layouts: 3.44 us -> 2.05 us
    concatenate x1 -> x0, other arithmetic: 0.59 us -> none  [on_device(): edges = jnp.concatenate([first, beyond])]
where the time goes in v2:
time: 40.3 us; the launch traced here: 40.1 us
  Pallas kernels  36.1 us (90%)
  local copies, waits for them, and re-layouts  2.05 us (5%)
  between operations  1.94 us (5%)
    pallas_call x1, Pallas kernels, on_device(): pl.pallas_call(functools.partial(kernel, sizes, cells), out_shape=(pltpu....  36.1 us
    unnamed x3, local copies, waits for them, and re-layouts  2.05 us

profile of v2, /device:TPU:1, one launch (start us, length us, event | category | flops | bytes accessed | tf_op | source)
XLA Modules:
  0.0 40.1 jit_solution(9258595930994017460)
XLA Ops:
  1.9 36.1 %shard_map.58 = (f32[32,64,128]{2,1,0:T(8,128)S(1)}, f32[256]{0:T(256)S(1)}, f32[4]{0:T(128)S(4)}) custom-call(f32[32,64,128]{2,1,0:T(8,128)} %u_hbm.1, s32[1]{0:T(128)S(6)} %copy.12.first_hbm, s32[1]{0:T(128)S(6)} %copy.13.beyond_hbm), custom_call_target="tpu_custom_call" | custom-call | tf_op jit(solution)/shard_map/pallas_call | solution.py:353
  38.1 1.0 %copy.9 = f32[32,64,128]{2,1,0:T(8,128)} copy(f32[32,64,128]{2,1,0:T(8,128)S(1)} %get-tuple-element.3) | data formatting | bytes 2097152
  39.0 0.5 %copy.11 = f32[4]{0:T(128)} copy(f32[4]{0:T(128)S(4)} %get-tuple-element.5) | data formatting | bytes 32
  39.6 0.6 %copy.10 = f32[256]{0:T(256)} copy(f32[256]{0:T(256)S(1)} %get-tuple-element.4) | data formatting | bytes 2048

commit v3 on v2

--- a/solution.py
+++ b/solution.py
@@ -10,7 +10,8 @@
 MESH = pl.DeviceIdType.MESH
 BINS = 256
 RANGE = 12.0
-COEF = (0.8, -0.2, 4.0 / 105.0, -1.0 / 280.0)
+SCALE = 0.8
+COEF = (1.0, -1.0 / 4.0, 1.0 / 21.0, -1.0 / 224.0)
 
 
 def pair(x):
@@ -37,8 +38,14 @@
     def signal(sem, **offset):
         pl.semaphore_signal(sem, inc=1, device_id=device(**offset), device_id_type=MESH)
 
-    load = pltpu.make_async_copy(u_hbm, ext.at[pl.ds(4, dz), pl.ds(8, dy), :], in_sem)
-    load.start()
+    loads = [
+        pltpu.make_async_copy(
+            u_hbm.at[pl.ds(z, 8)], ext.at[pl.ds(4 + z, 8), pl.ds(8, dy), :], in_sem.at[z // 8]
+        )
+        for z in range(0, dz, 8)
+    ]
+    for load in loads:
+        load.start()
     barrier = pltpu.get_barrier_semaphore()
     for offset in (dict(a=-1), dict(a=1), dict(c=-1), dict(c=1), dict(b=-1), dict(b=1)):
         signal(barrier, **offset)
@@ -52,23 +59,20 @@
     lane = lax.broadcasted_iota(jnp.int32, (8, dx), 1)
     slot = lane // 8
     left_rim = lane % 8 < 4
-    lane16 = lax.broadcasted_iota(jnp.int32, (16, dx), 1)
-    half = (lax.broadcasted_iota(jnp.int32, (16, dx), 0) // 8).astype(jnp.float32)
-    half_core = jnp.where((lane16 < 4) | (lane16 >= dx - 4), 1000.0, half)
     rim_lane = (lane < 4) | (lane >= dx - 4)
-
-    load.wait()
-
-    def pack(i, _):
-        for p in (4 * i, 4 * i + 1, 4 * i + 2, 4 * i + 3):
+    top = jnp.full((8, dx), BINS - 2.0, jnp.float32)
+    core_top = jnp.where(rim_lane, -32.0, top)
+    spread = (lax.broadcasted_iota(jnp.int32, (8, dx), 0) * dx + lane) * 389 % 1024
+    spread = (spread.astype(jnp.float32) + 0.5) * (1.0 / 1024.0)
+
+    for i, load in enumerate(loads):
+        load.wait()
+        for p in range(4 * i, 4 * i + 4):
             out = jnp.zeros((8, dx), jnp.float32)
             for j in range(16):
                 cell = ext[4 + 2 * p + j // 8, pl.ds(8 + 8 * (j % 8), 8), :]
                 out = jnp.where(slot == j, pltpu.roll(cell, 8 * j + 4, 1), out)
             packed[p] = out
-        return 0
-
-    lax.fori_loop(0, dz // 8, pack, 0)
 
     pl.semaphore_wait(barrier, 6)
 
@@ -98,45 +102,44 @@
     low_edge = first[0].astype(jnp.float32) - 1.0
     high_edge = beyond[0].astype(jnp.float32) - 1.0
 
-    def classify(square, halves, stats):
+    def classify(square, last, stats):
         wsum, wmax, wmin = stats
-        magnitude = jnp.sqrt(square + 1.0) - 1.0
+        root = square * (SCALE * SCALE) + 1.0
+        magnitude = root * lax.rsqrt(root) - 1.0
         place = jnp.clip(magnitude * (BINS / RANGE) - 0.5, 0.0, BINS - 1.0)
-        low = jnp.minimum(jnp.floor(place), BINS - 2.0)
-        fraction = place - low
+        low = jnp.minimum(jnp.floor(place), last)
+        share = jnp.floor((place - low) * 256.0 + spread)
         weight = jnp.clip(place - low_edge, 0.0, 1.0) - jnp.clip(place - high_edge, 0.0, 1.0)
         value = weight * magnitude
         stats = (
             wsum + value,
             jnp.maximum(wmax, value),
-            jnp.minimum(wmin, (magnitude + RANGE) - RANGE * weight),
-        )
-        coarse = jnp.floor(low * 0.125)
-        fine = low - 8.0 * coarse
-        coarse = (pair(coarse) - halves).astype(jnp.bfloat16)
-        fine = (pair(fine) - half).astype(jnp.bfloat16)
-        part = fraction.astype(jnp.bfloat16)
-        rest = (fraction - part.astype(jnp.float32)).astype(jnp.bfloat16)
-        part, rest = pair(part), pair(rest)
+            jnp.minimum(wmin, magnitude - RANGE * weight),
+        )
+        coarse = jnp.floor(low * 0.0625)
+        fine = low - 16.0 * coarse
+        coarse = jnp.concatenate([coarse, coarse - 1.0], axis=0).astype(jnp.bfloat16)
+        fine = jnp.concatenate([fine, fine - 1.0], axis=0).astype(jnp.bfloat16)
+        share = pair(share).astype(jnp.bfloat16)
         one = jnp.ones((16, dx), jnp.bfloat16)
         zero = jnp.zeros((16, dx), jnp.bfloat16)
-        left = jnp.concatenate(
-            [jnp.where(coarse == jnp.bfloat16(2 * k), one, zero) for k in range(16)], axis=0
-        )
-        hits = [fine == jnp.bfloat16(2 * k) for k in range(4)]
-        right = jnp.concatenate(
-            [jnp.where(hit, term, zero) for term in (one, part, rest) for hit in hits], axis=0
-        )
-        return magnitude, left, right, stats
-
-    def count(lefts, rights):
+        coarse_hot = jnp.concatenate(
+            [jnp.where(coarse == jnp.bfloat16(2 * k), one, zero) for k in range(8)], axis=0
+        )
+        hits = [fine == jnp.bfloat16(2 * k) for k in range(8)]
+        fine_hot = jnp.concatenate(
+            [jnp.where(hit, term, zero) for term in (one, share) for hit in hits], axis=0
+        )
+        return magnitude, fine_hot, coarse_hot, stats
+
+    def count(fines, coarses):
         acc[...] += lax.dot_general(
-            jnp.concatenate(lefts, axis=1), jnp.concatenate(rights, axis=1),
+            jnp.concatenate(coarses, axis=1), jnp.concatenate(fines, axis=1),
             (((1,), (1,)), ((), ())), preferred_element_type=jnp.float32,
         )
 
     def tiles(pairs, stats, fresh):
-        lefts, rights = [], []
+        fines, coarses = [], []
         for p, which in pairs:
             if fresh:
                 out_x = jnp.zeros((8, dx), jnp.float32)
@@ -146,26 +149,25 @@
             for j in which:
                 z, y = 4 + 2 * p + j // 8, 8 + 8 * (j % 8)
                 center = ext[z, pl.ds(y, 8), :]
-                grad_x = grad_y = grad_z = None
                 for k, coef in enumerate(COEF, start=1):
-                    term_x = coef * (pltpu.roll(center, dx - k, 1) - pltpu.roll(center, k, 1))
-                    term_y = coef * (ext[z, pl.ds(y + k, 8), :] - ext[z, pl.ds(y - k, 8), :])
-                    term_z = coef * (ext[z + k, pl.ds(y, 8), :] - ext[z - k, pl.ds(y, 8), :])
-                    grad_x = term_x if grad_x is None else grad_x + term_x
-                    grad_y = term_y if grad_y is None else grad_y + term_y
-                    grad_z = term_z if grad_z is None else grad_z + term_z
+                    term_x = pltpu.roll(center, dx - k, 1) - pltpu.roll(center, k, 1)
+                    term_y = ext[z, pl.ds(y + k, 8), :] - ext[z, pl.ds(y - k, 8), :]
+                    term_z = ext[z + k, pl.ds(y, 8), :] - ext[z - k, pl.ds(y, 8), :]
+                    grad_x = term_x if k == 1 else grad_x + coef * term_x
+                    grad_y = term_y if k == 1 else grad_y + coef * term_y
+                    grad_z = term_z if k == 1 else grad_z + coef * term_z
                 square_yz = grad_z * grad_z + grad_y * grad_y
                 out_x = jnp.where(slot == j, pltpu.roll(grad_x, 8 * j + 4, 1), out_x)
                 out_yz = jnp.where(slot == j, pltpu.roll(square_yz, 8 * j + 4, 1), out_yz)
-                magnitude, left, right, stats = classify(
-                    square_yz + grad_x * grad_x, half_core, stats
+                magnitude, fine_hot, coarse_hot, stats = classify(
+                    square_yz + grad_x * grad_x, core_top, stats
                 )
                 mag_ref[2 * p + j // 8, pl.ds(8 * (j % 8), 8), :] = magnitude
-                lefts.append(left)
-                rights.append(right)
+                fines.append(fine_hot)
+                coarses.append(coarse_hot)
             rim_x[p] = out_x
             rim_yz[p] = out_yz
-        count(lefts, rights)
+        count(fines, coarses)
         return stats
 
     inner = [j for j in range(16) if 0 < j % 8 < 7]
@@ -174,8 +176,8 @@
     stats = (nothing, nothing, jnp.full((8, dx), 1e30, jnp.float32))
 
     stats = lax.fori_loop(
-        0, (dz - 8) // 4,
-        lambda i, s: tiles([(2 + 2 * i, inner), (3 + 2 * i, inner)], s, True), stats,
+        0, (dz - 8) // 8,
+        lambda i, s: tiles([(2 + 4 * i + k, inner) for k in range(4)], s, True), stats,
     )
 
     for copy in y_rims:
@@ -185,8 +187,10 @@
         signal(far2, c=-2)
         signal(far2, c=2)
     stats = lax.fori_loop(
-        0, (dz - 8) // 8,
-        lambda i, s: tiles([(2 + 4 * i + k, outer) for k in range(4)], s, False), stats,
+        0, 2,
+        lambda i, s: tiles(
+            [(2 + (dz - 8) // 4 * i + k, outer) for k in range((dz - 8) // 4)], s, False
+        ), stats,
     )
 
     for copy in xz_rims:
@@ -201,8 +205,8 @@
         signal(near2, b=2)
         signal(near2, a=2)
     stats = lax.fori_loop(
-        0, 4,
-        lambda i, s: tiles([(i + (dz // 2 - 4) * (i // 2), range(16))], s, True), stats,
+        0, 2,
+        lambda i, s: tiles([(k + (dz // 2 - 2) * i, range(16)) for k in range(2)], s, True), stats,
     )
     if nz > 4:
         pl.semaphore_wait(near2, 3)
@@ -210,29 +214,23 @@
 
     rim_stats = (nothing, nothing, jnp.full((8, dx), 1e30, jnp.float32))
 
-    def rims(i, rim_stats):
-        lefts, rights = [], []
-        for p in [8 * i + k for k in range(8)]:
-            own = packed[p]
-            high = jnp.where(left_rim, 0.0, from_high[p] - own)
-            low = jnp.where(left_rim, from_low[p] - own, 0.0)
-            fix_high = fix_low = None
-            for k, coef in enumerate(COEF, start=1):
-                more = coef * pltpu.roll(high, dx - k, 1)
-                less = coef * pltpu.roll(low, k, 1)
-                fix_high = more if fix_high is None else fix_high + more
-                fix_low = less if fix_low is None else fix_low + less
-            grad_x = rim_x[p] + jnp.where(left_rim, fix_high, -fix_low)
-            magnitude, left, right, rim_stats = classify(
-                rim_yz[p] + grad_x * grad_x, half, rim_stats
-            )
-            rim_x[p] = magnitude
-            lefts.append(left)
-            rights.append(right)
-        count(lefts, rights)
-        return rim_stats
-
-    rim_stats = lax.fori_loop(0, dz // 16, rims, rim_stats)
+    fines, coarses = [], []
+    for p in range(dz // 2):
+        own = packed[p]
+        high = jnp.where(left_rim, 0.0, from_high[p] - own)
+        low = jnp.where(left_rim, from_low[p] - own, 0.0)
+        fix_high = fix_low = None
+        for k, coef in enumerate(COEF, start=1):
+            more = coef * pltpu.roll(high, dx - k, 1)
+            less = coef * pltpu.roll(low, k, 1)
+            fix_high = more if fix_high is None else fix_high + more
+            fix_low = less if fix_low is None else fix_low + less
+        grad_x = rim_x[p] + jnp.where(left_rim, fix_high, -fix_low)
+        magnitude, fine_hot, coarse_hot, rim_stats = classify(rim_yz[p] + grad_x * grad_x, top, rim_stats)
+        rim_x[p] = magnitude
+        fines.append(fine_hot)
+        coarses.append(coarse_hot)
+    count(fines, coarses)
 
     wsum = rim_stats[0] + jnp.where(rim_lane, 0.0, stats[0])
     wmax = jnp.maximum(rim_stats[1], jnp.where(rim_lane, 0.0, stats[1]))
@@ -243,31 +241,29 @@
         lax.broadcasted_iota(jnp.int32, total.shape, 0) % 8
         == lax.broadcasted_iota(jnp.int32, total.shape, 1) % 8
     )
-    total = jnp.where(same, total, 0.0).reshape(32, 8, 192).sum(axis=1)
-    source = lax.broadcasted_iota(jnp.int32, (192, 128), 0)
-    target = lax.broadcasted_iota(jnp.int32, (192, 128), 1)
-    fits = (source // 8) % 8 == target % 8
-    coarse_row = lax.broadcasted_iota(jnp.int32, (32, 128), 0)
-    coarse_lane = lax.broadcasted_iota(jnp.int32, (32, 128), 1)
-    keep = coarse_row % 16 == coarse_lane // 8
-
-    def bins_of(chosen):
-        spread = lax.dot_general(
-            total, jnp.where(fits & chosen, 1.0, 0.0), (((1,), (0,)), ((), ())),
-            precision=lax.Precision.HIGHEST, preferred_element_type=jnp.float32,
-        )
-        spread = jnp.where(keep, spread, 0.0)
-        return spread[:16].sum(axis=0, keepdims=True), spread[16:].sum(axis=0, keepdims=True)
-
-    number = bins_of(source < 64)
-    part = bins_of(source >= 64)
+    total = jnp.where(same, total, 0.0).reshape(16, 8, 256).sum(axis=1)
+    source = lax.broadcasted_iota(jnp.int32, (256, 256), 0)
+    target = lax.broadcasted_iota(jnp.int32, (256, 256), 1)
+    fits = (source // 128 == target // 128) & ((source // 8) % 16 == target % 16)
+    total = lax.dot_general(
+        total, jnp.where(fits, 1.0, 0.0), (((1,), (0,)), ((), ())),
+        precision=lax.Precision.HIGHEST, preferred_element_type=jnp.float32,
+    )
+    keep = (
+        lax.broadcasted_iota(jnp.int32, (16, 256), 0) % 8
+        == (lax.broadcasted_iota(jnp.int32, (16, 256), 1) % 128) // 16
+    )
+    total = jnp.where(keep, total, 0.0)
+    halves = [x.sum(axis=0, keepdims=True) for x in (total[:8], total[8:])]
+    number = [x[:, :128] for x in halves]
+    part = [x[:, 128:] * (1.0 / 256.0) for x in halves]
     lane1 = lane[:1]
     turned = [pltpu.roll(pair(pair(pair(x))), 1, 1)[:1] for x in part]
     row0 = number[0] - part[0] + jnp.where(lane1 == 0, turned[1], turned[0])
     row1 = number[1] - part[1] + jnp.where(lane1 == 0, turned[0], turned[1])
     row2 = jnp.where(
         lane1 == 0, jnp.sum(wsum),
-        jnp.where(lane1 == 1, jnp.max(wmax), jnp.min(wmin)),
+        jnp.where(lane1 == 1, jnp.max(wmax), jnp.min(wmin) + RANGE),
     )
     msg[0:3, :] = jnp.concatenate([row0, row1, row2], axis=0)
 
@@ -342,6 +338,21 @@
     stat_ref[3] = number * (1.0 / cells)
 
 
+def write_out(mag, hist, stat, mag_hbm, hist_hbm, stat_hbm, sems):
+    step = mag.shape[0] // 4
+    copies = [
+        pltpu.make_async_copy(hist, hist_hbm, sems.at[0]),
+        pltpu.make_async_copy(stat, stat_hbm, sems.at[1]),
+    ]
+    for k in range(4):
+        part = pl.ds(step * k, step)
+        copies.append(pltpu.make_async_copy(mag.at[part], mag_hbm.at[part], sems.at[2 + k]))
+    for copy in copies:
+        copy.start()
+    for copy in copies:
+        copy.wait()
+
+
 def solution(mesh):
     sizes = tuple(mesh.shape[name] for name in ("gx", "gy", "gz"))
     nx, ny, nz = sizes
@@ -350,7 +361,7 @@
         dz, dy, dx = u.shape
         cells = u.size * nx * ny * nz
         rims = pltpu.VMEM((dz // 2, 8, dx), jnp.float32)
-        return pl.pallas_call(
+        mag, hist, stat = pl.pallas_call(
             functools.partial(kernel, sizes, cells),
             out_shape=(
                 pltpu.VMEM(u.shape, jnp.float32),
@@ -366,13 +377,13 @@
             scratch_shapes=[
                 pltpu.VMEM((dz + 8, dy + 16, dx), jnp.float32),
                 rims, rims, rims, rims, rims,
-                pltpu.VMEM((256, 192), jnp.float32),
+                pltpu.VMEM((128, 256), jnp.float32),
                 pltpu.VMEM((3, 128), jnp.float32),
                 pltpu.VMEM((nx * nz, 3, 128), jnp.float32),
                 pltpu.VMEM((ny, 3, 128), jnp.float32),
                 pltpu.SMEM((1,), jnp.int32),
                 pltpu.SMEM((1,), jnp.int32),
-                pltpu.SemaphoreType.DMA,
+                pltpu.SemaphoreType.DMA((dz // 8,)),
                 pltpu.SemaphoreType.DMA((2,)),
                 pltpu.SemaphoreType.DMA((6,)),
                 pltpu.SemaphoreType.DMA((6,)),
@@ -387,6 +398,23 @@
             ],
             compiler_params=pltpu.CompilerParams(collective_id=0, has_side_effects=True),
         )(u, first, beyond)
+        mag = pltpu.with_memory_space_constraint(mag, pltpu.VMEM)
+        hist = pltpu.with_memory_space_constraint(hist, pltpu.VMEM)
+        return pl.pallas_call(
+            write_out,
+            out_shape=(
+                jax.ShapeDtypeStruct(u.shape, jnp.float32),
+                jax.ShapeDtypeStruct((BINS,), jnp.float32),
+                jax.ShapeDtypeStruct((4,), jnp.float32),
+            ),
+            in_specs=[
+                pl.BlockSpec(memory_space=pltpu.VMEM),
+                pl.BlockSpec(memory_space=pltpu.VMEM),
+                pl.BlockSpec(memory_space=pltpu.SMEM),
+            ],
+            out_specs=[pl.BlockSpec(memory_space=pltpu.HBM)] * 3,
+            scratch_shapes=[pltpu.SemaphoreType.DMA((6,))],
+        )(mag, hist, stat)
 
     return jax.shard_map(
         on_device,

time: 40.3 us -> 38.7 us (0.960)
  local copies, waits for them, and re-layouts: 2.05 us -> 0 us
  Pallas kernels: 36.1 us -> 36.6 us
    unnamed x3 -> x0, local copies, waits for them, and re-layouts: 2.05 us -> none
    pallas_call x0 -> x1, Pallas kernels: none -> 1.02 us  [on_device(): pl.pallas_call(write_out, out_shape=(jax.ShapeDtypeStruct(u.shape, jnp.fl...]
    pallas_call x1, Pallas kernels: 36.1 us -> 35.6 us  [on_device(): pl.pallas_call(functools.partial(kernel, sizes, cells), out_shape=(pltpu....]
where the time goes in v3:
time: 38.7 us; the launch traced here: 38.5 us
  Pallas kernels  36.6 us (95%)
  between operations  1.93 us (5%)
    pallas_call x1, Pallas kernels, on_device(): pl.pallas_call(functools.partial(kernel, sizes, cells), out_shape=(pltpu....  35.6 us
    pallas_call x1, Pallas kernels, on_device(): pl.pallas_call(write_out, out_shape=(jax.ShapeDtypeStruct(u.shape, jnp.fl...  1.02 us

profile of v3, /device:TPU:1, one launch (start us, length us, event | category | flops | bytes accessed | tf_op | source)
XLA Modules:
  0.0 38.5 jit_solution(12152062637727288853)
XLA Ops:
  1.9 35.6 %shard_map.58 = (f32[32,64,128]{2,1,0:T(8,128)S(1)}, f32[256]{0:T(256)S(1)}, f32[4]{0:T(128)S(4)}) custom-call(f32[32,64,128]{2,1,0:T(8,128)} %u_hbm.1, s32[1]{0:T(128)S(6)} %copy.6.first_hbm, s32[1]{0:T(128)S(6)} %copy.7.beyond_hbm), custom_call_target="tpu_custom_call" | custom-call | tf_op jit(solution)/shard_map/pallas_call | solution.py:364
  37.5 1.0 %shard_map.59 = (f32[32,64,128]{2,1,0:T(8,128)}, f32[256]{0:T(256)}, f32[4]{0:T(128)}) custom-call(f32[32,64,128]{2,1,0:T(8,128)S(1)} %get-tuple-element.6.mag, f32[256]{0:T(256)S(1)} %get-tuple-element.7.hist, f32[4]{0:T(128)S(4)} %get-tuple-element.8.stat), custom_call_target="tpu_custom_call" | custom-call | tf_op jit(solution)/shard_map/pallas_call | solution.py:403

commit v4 on v3

--- a/solution.py
+++ b/solution.py
@@ -20,9 +20,9 @@
 
 def kernel(
     sizes, cells, u_hbm, first_hbm, beyond_hbm, mag_ref, hist_ref, stat_ref,
-    ext, packed, from_low, from_high, rim_x, rim_yz, acc, msg, plane, line, first, beyond,
+    ext, packed, to_low, to_high, from_low, from_high, rim_x, rim_yz, acc, msg, plane, line, first, beyond,
     in_sem, edge_sem, send_sem, recv_sem, plane_send, plane_recv, line_send, line_recv,
-    near2, near3, far2, far3,
+    hop1, near2, near3, far2, far3,
 ):
     nx, ny, nz = sizes
     dz, dy, dx = u_hbm.shape
@@ -42,12 +42,13 @@
         pltpu.make_async_copy(
             u_hbm.at[pl.ds(z, 8)], ext.at[pl.ds(4 + z, 8), pl.ds(8, dy), :], in_sem.at[z // 8]
         )
-        for z in range(0, dz, 8)
+        for z in sorted(range(0, dz, 8), key=lambda z: min(z, dz - 8 - z))
     ]
     for load in loads:
         load.start()
     barrier = pltpu.get_barrier_semaphore()
-    for offset in (dict(a=-1), dict(a=1), dict(c=-1), dict(c=1), dict(b=-1), dict(b=1)):
+    neighbours = (dict(a=-1), dict(a=1), dict(b=-1), dict(b=1), dict(c=-1), dict(c=1))
+    for offset in neighbours:
         signal(barrier, **offset)
     edge_loads = [
         pltpu.make_async_copy(first_hbm, first, edge_sem.at[0]),
@@ -60,77 +61,92 @@
     slot = lane // 8
     left_rim = lane % 8 < 4
     rim_lane = (lane < 4) | (lane >= dx - 4)
-    top = jnp.full((8, dx), BINS - 2.0, jnp.float32)
-    core_top = jnp.where(rim_lane, -32.0, top)
+    top = jnp.full((8, dx), BINS // 2 - 1.0, jnp.float32)
+    core_top = jnp.where(rim_lane, -64.0, top)
     spread = (lax.broadcasted_iota(jnp.int32, (8, dx), 0) * dx + lane) * 389 % 1024
     spread = (spread.astype(jnp.float32) + 0.5) * (1.0 / 1024.0)
 
-    for i, load in enumerate(loads):
+    def send(k, src, dst, **offset):
+        copy = pltpu.make_async_remote_copy(
+            src_ref=src, dst_ref=dst, send_sem=send_sem.at[k], recv_sem=recv_sem.at[k],
+            device_id=device(**offset), device_id_type=MESH,
+        )
+        copy.start()
+        return copy
+
+    rows = pl.ds(8, dy)
+    planes = pl.ds(4, dz)
+    for load in loads[:2]:
         load.wait()
-        for p in range(4 * i, 4 * i + 4):
+    pl.semaphore_wait(barrier, 6)
+    z_rims = [
+        send(0, ext.at[pl.ds(4, 4), rows, :], ext.at[pl.ds(4 + dz, 4), rows, :], b=-1),
+        send(1, ext.at[pl.ds(dz, 4), rows, :], ext.at[pl.ds(0, 4), rows, :], b=1),
+    ]
+    for load in loads[2:]:
+        load.wait()
+    y_rims = [
+        send(2, ext.at[planes, pl.ds(8, 4), :], ext.at[planes, pl.ds(8 + dy, 4), :], c=-1),
+        send(3, ext.at[planes, pl.ds(4 + dy, 4), :], ext.at[planes, pl.ds(4, 4), :], c=1),
+    ]
+    for offset in neighbours:
+        signal(hop1, **offset)
+    for m in range(dz // 4):
+        both = []
+        for p in (2 * m, 2 * m + 1):
             out = jnp.zeros((8, dx), jnp.float32)
             for j in range(16):
                 cell = ext[4 + 2 * p + j // 8, pl.ds(8 + 8 * (j % 8), 8), :]
                 out = jnp.where(slot == j, pltpu.roll(cell, 8 * j + 4, 1), out)
             packed[p] = out
-
-    pl.semaphore_wait(barrier, 6)
-
-    def send(k, src, dst, **offset):
-        copy = pltpu.make_async_remote_copy(
-            src_ref=src, dst_ref=dst, send_sem=send_sem.at[k], recv_sem=recv_sem.at[k],
-            device_id=device(**offset), device_id_type=MESH,
-        )
-        copy.start()
-        return copy
-
-    rows = pl.ds(8, dy)
-    planes = pl.ds(4, dz)
-    y_rims = [
-        send(0, ext.at[planes, pl.ds(8, 4), :], ext.at[planes, pl.ds(8 + dy, 4), :], c=-1),
-        send(1, ext.at[planes, pl.ds(4 + dy, 4), :], ext.at[planes, pl.ds(4, 4), :], c=1),
-    ]
-    xz_rims = [
-        send(4, ext.at[pl.ds(4, 4), rows, :], ext.at[pl.ds(4 + dz, 4), rows, :], b=-1),
-        send(5, ext.at[pl.ds(dz, 4), rows, :], ext.at[pl.ds(0, 4), rows, :], b=1),
-        send(2, packed, from_high, a=-1),
-        send(3, packed, from_low, a=1),
+            both.append(out)
+        to_high[m] = jnp.where(left_rim, both[0], pltpu.roll(both[1], 4, 1))
+        to_low[m] = jnp.where(left_rim, pltpu.roll(both[0], dx - 4, 1), both[1])
+    x_rims = [
+        send(4, to_low, from_high, a=-1),
+        send(5, to_high, from_low, a=1),
     ]
     acc[...] = jnp.zeros_like(acc)
     for copy in edge_loads:
         copy.wait()
-    low_edge = first[0].astype(jnp.float32) - 1.0
-    high_edge = beyond[0].astype(jnp.float32) - 1.0
+    low_edge = first[0].astype(jnp.float32) * 0.5 - 0.5
+    high_edge = beyond[0].astype(jnp.float32) * 0.5 - 0.5
 
     def classify(square, last, stats):
         wsum, wmax, wmin = stats
         root = square * (SCALE * SCALE) + 1.0
         magnitude = root * lax.rsqrt(root) - 1.0
-        place = jnp.clip(magnitude * (BINS / RANGE) - 0.5, 0.0, BINS - 1.0)
+        place = jnp.clip(magnitude * (0.5 * BINS / RANGE) - 0.25, 0.0, 0.5 * BINS - 0.5)
         low = jnp.minimum(jnp.floor(place), last)
-        share = jnp.floor((place - low) * 256.0 + spread)
-        weight = jnp.clip(place - low_edge, 0.0, 1.0) - jnp.clip(place - high_edge, 0.0, 1.0)
+        share = jnp.floor((place - low) * 512.0 + spread)
+        weight = jnp.clip(place - low_edge, 0.0, 0.5) - jnp.clip(place - high_edge, 0.0, 0.5)
         value = weight * magnitude
         stats = (
             wsum + value,
             jnp.maximum(wmax, value),
-            jnp.minimum(wmin, magnitude - RANGE * weight),
-        )
-        coarse = jnp.floor(low * 0.0625)
-        fine = low - 16.0 * coarse
+            jnp.minimum(wmin, magnitude - (2.0 * RANGE) * weight),
+        )
+        coarse = jnp.floor(low * 0.125)
+        fine = low - 8.0 * coarse
         coarse = jnp.concatenate([coarse, coarse - 1.0], axis=0).astype(jnp.bfloat16)
-        fine = jnp.concatenate([fine, fine - 1.0], axis=0).astype(jnp.bfloat16)
-        share = pair(share).astype(jnp.bfloat16)
+        fine = pair(fine).astype(jnp.bfloat16)
+        here = jnp.concatenate(
+            [jnp.maximum(256.0 - share, 0.0), jnp.minimum(share, 512.0 - share)], axis=0
+        ).astype(jnp.bfloat16)
+        after = jnp.concatenate(
+            [jnp.maximum(share - 256.0, 0.0), jnp.zeros((8, dx), jnp.float32)], axis=0
+        ).astype(jnp.bfloat16)
         one = jnp.ones((16, dx), jnp.bfloat16)
         zero = jnp.zeros((16, dx), jnp.bfloat16)
         coarse_hot = jnp.concatenate(
             [jnp.where(coarse == jnp.bfloat16(2 * k), one, zero) for k in range(8)], axis=0
         )
-        hits = [fine == jnp.bfloat16(2 * k) for k in range(8)]
-        fine_hot = jnp.concatenate(
-            [jnp.where(hit, term, zero) for term in (one, share) for hit in hits], axis=0
-        )
-        return magnitude, fine_hot, coarse_hot, stats
+        hits = [fine == jnp.bfloat16(k) for k in range(8)]
+        parts = [jnp.where(hits[0], here, zero)]
+        for k in range(1, 8):
+            parts.append(jnp.where(hits[k], here, jnp.where(hits[k - 1], after, zero)))
+        parts.append(jnp.where(hits[7], after, zero))
+        return magnitude, jnp.concatenate(parts, axis=0), coarse_hot, stats
 
     def count(fines, coarses):
         acc[...] += lax.dot_general(
@@ -175,50 +191,62 @@
     nothing = jnp.zeros((8, dx), jnp.float32)
     stats = (nothing, nothing, jnp.full((8, dx), 1e30, jnp.float32))
 
-    stats = lax.fori_loop(
-        0, (dz - 8) // 8,
-        lambda i, s: tiles([(2 + 4 * i + k, inner) for k in range(4)], s, True), stats,
-    )
+    def trips(count_of, pairs, which, stats, fresh):
+        step = len(pairs) // count_of
+        if count_of == 1:
+            return tiles([(p, which) for p in pairs], stats, fresh)
+        gap = pairs[step] - pairs[0]
+        return lax.fori_loop(
+            0, count_of, lambda i, s: tiles([(p + gap * i, which) for p in pairs[:step]], s, fresh), stats
+        )
+
+    middle = list(range(2, dz // 2 - 2))
+    ends = [0, 1, dz // 2 - 2, dz // 2 - 1]
+
+    stats = trips(3, middle, inner, stats, True)
+
+    pl.semaphore_wait(hop1, 6)
+    if nz > 4:
+        signal(near2, b=-2)
+        signal(near2, b=2)
+        signal(near2, a=2)
+    if ny > 4:
+        signal(far2, c=-2)
+        signal(far2, c=2)
 
     for copy in y_rims:
         copy.wait_send()
         copy.wait_recv()
-    if ny > 4:
-        signal(far2, c=-2)
-        signal(far2, c=2)
-    stats = lax.fori_loop(
-        0, 2,
-        lambda i, s: tiles(
-            [(2 + (dz - 8) // 4 * i + k, outer) for k in range((dz - 8) // 4)], s, False
-        ), stats,
-    )
-
-    for copy in xz_rims:
+    stats = trips(1, middle, outer, stats, False)
+
+    for copy in z_rims:
         copy.wait_send()
         copy.wait_recv()
+    stats = trips(2, ends, list(range(16)), stats, True)
+
+    if nz > 4:
+        pl.semaphore_wait(near2, 3)
+        signal(near3, b=4)
     if ny > 4:
         pl.semaphore_wait(far2, 2)
         signal(far3, c=-4)
         signal(far3, c=4)
-    if nz > 4:
-        signal(near2, b=-2)
-        signal(near2, b=2)
-        signal(near2, a=2)
-    stats = lax.fori_loop(
-        0, 2,
-        lambda i, s: tiles([(k + (dz // 2 - 2) * i, range(16)) for k in range(2)], s, True), stats,
-    )
-    if nz > 4:
-        pl.semaphore_wait(near2, 3)
-        signal(near3, b=4)
 
     rim_stats = (nothing, nothing, jnp.full((8, dx), 1e30, jnp.float32))
 
+    for copy in x_rims:
+        copy.wait_send()
+        copy.wait_recv()
     fines, coarses = [], []
     for p in range(dz // 2):
         own = packed[p]
-        high = jnp.where(left_rim, 0.0, from_high[p] - own)
-        low = jnp.where(left_rim, from_low[p] - own, 0.0)
+        high, low = from_high[p // 2], from_low[p // 2]
+        if p % 2:
+            low = pltpu.roll(low, dx - 4, 1)
+        else:
+            high = pltpu.roll(high, 4, 1)
+        high = jnp.where(left_rim, 0.0, high - own)
+        low = jnp.where(left_rim, low - own, 0.0)
         fix_high = fix_low = None
         for k, coef in enumerate(COEF, start=1):
             more = coef * pltpu.roll(high, dx - k, 1)
@@ -241,29 +269,32 @@
         lax.broadcasted_iota(jnp.int32, total.shape, 0) % 8
         == lax.broadcasted_iota(jnp.int32, total.shape, 1) % 8
     )
-    total = jnp.where(same, total, 0.0).reshape(16, 8, 256).sum(axis=1)
-    source = lax.broadcasted_iota(jnp.int32, (256, 256), 0)
-    target = lax.broadcasted_iota(jnp.int32, (256, 256), 1)
-    fits = (source // 128 == target // 128) & ((source // 8) % 16 == target % 16)
+    total = jnp.where(same, total, 0.0).reshape(16, 8, 144).sum(axis=1)
+    source = lax.broadcasted_iota(jnp.int32, (144, 256), 0) // 8
+    target = lax.broadcasted_iota(jnp.int32, (144, 256), 1)
+    fits = (source == target % 16 + 16 * (target // 128)).astype(jnp.float32).astype(jnp.bfloat16)
+    pieces = []
+    for _ in range(3):
+        pieces.append(total.astype(jnp.bfloat16))
+        total = total - pieces[-1].astype(jnp.float32)
     total = lax.dot_general(
-        total, jnp.where(fits, 1.0, 0.0), (((1,), (0,)), ((), ())),
-        precision=lax.Precision.HIGHEST, preferred_element_type=jnp.float32,
-    )
-    keep = (
-        lax.broadcasted_iota(jnp.int32, (16, 256), 0) % 8
-        == (lax.broadcasted_iota(jnp.int32, (16, 256), 1) % 128) // 16
-    )
-    total = jnp.where(keep, total, 0.0)
-    halves = [x.sum(axis=0, keepdims=True) for x in (total[:8], total[8:])]
-    number = [x[:, :128] for x in halves]
-    part = [x[:, 128:] * (1.0 / 256.0) for x in halves]
+        jnp.concatenate(pieces, axis=0), fits, (((1,), (0,)), ((), ())),
+        preferred_element_type=jnp.float32,
+    )
+    total = total[:16] + total[16:32] + total[32:]
+    owner = lax.broadcasted_iota(jnp.int32, (16, 128), 1) // 16
+    coarse = lax.broadcasted_iota(jnp.int32, (16, 128), 0)
+
+    def bin_row(r):
+        mine = jnp.where(coarse == owner + 8 * r, total[:, :128], 0.0)
+        carried = jnp.where(coarse + 1 == owner + 8 * r, total[:, 128:], 0.0)
+        return (mine + carried).sum(axis=0, keepdims=True) * (1.0 / 256.0)
+
+    row0, row1 = bin_row(0), bin_row(1)
     lane1 = lane[:1]
-    turned = [pltpu.roll(pair(pair(pair(x))), 1, 1)[:1] for x in part]
-    row0 = number[0] - part[0] + jnp.where(lane1 == 0, turned[1], turned[0])
-    row1 = number[1] - part[1] + jnp.where(lane1 == 0, turned[0], turned[1])
     row2 = jnp.where(
-        lane1 == 0, jnp.sum(wsum),
-        jnp.where(lane1 == 1, jnp.max(wmax), jnp.min(wmin) + RANGE),
+        lane1 == 0, jnp.sum(wsum) * 2.0,
+        jnp.where(lane1 == 1, jnp.max(wmax) * 2.0, jnp.min(wmin) + RANGE),
     )
     msg[0:3, :] = jnp.concatenate([row0, row1, row2], axis=0)
 
@@ -361,6 +392,7 @@
         dz, dy, dx = u.shape
         cells = u.size * nx * ny * nz
         rims = pltpu.VMEM((dz // 2, 8, dx), jnp.float32)
+        half_rims = pltpu.VMEM((dz // 4, 8, dx), jnp.float32)
         mag, hist, stat = pl.pallas_call(
             functools.partial(kernel, sizes, cells),
             out_shape=(
@@ -376,8 +408,8 @@
             ),
             scratch_shapes=[
                 pltpu.VMEM((dz + 8, dy + 16, dx), jnp.float32),
-                rims, rims, rims, rims, rims,
-                pltpu.VMEM((128, 256), jnp.float32),
+                rims, half_rims, half_rims, half_rims, half_rims, rims, rims,
+                pltpu.VMEM((128, 144), jnp.float32),
                 pltpu.VMEM((3, 128), jnp.float32),
                 pltpu.VMEM((nx * nz, 3, 128), jnp.float32),
                 pltpu.VMEM((ny, 3, 128), jnp.float32),
@@ -391,6 +423,7 @@
                 pltpu.SemaphoreType.DMA,
                 pltpu.SemaphoreType.DMA,
                 pltpu.SemaphoreType.DMA,
+                pltpu.SemaphoreType.REGULAR,
                 pltpu.SemaphoreType.REGULAR,
                 pltpu.SemaphoreType.REGULAR,
                 pltpu.SemaphoreType.REGULAR,

time: 38.7 us -> 37 us (0.956)
  Pallas kernels: 36.6 us -> 34.9 us
    pallas_call x1, Pallas kernels: 35.6 us -> 33.9 us  [on_device(): pl.pallas_call(functools.partial(kernel, sizes, cells), out_shape=(pltpu....]
where the time goes in v4:
time: 37 us; the launch traced here: 36.8 us
  Pallas kernels  34.9 us (94%)
  between operations  1.93 us (5%)
    pallas_call x1, Pallas kernels, on_device(): pl.pallas_call(functools.partial(kernel, sizes, cells), out_shape=(pltpu....  33.9 us
    pallas_call x1, Pallas kernels, on_device(): pl.pallas_call(write_out, out_shape=(jax.ShapeDtypeStruct(u.shape, jnp.fl...  1.02 us

profile of v4, /device:TPU:1, one launch (start us, length us, event | category | flops | bytes accessed | tf_op | source)
XLA Modules:
  0.0 36.8 jit_solution(13289184844577777145)
XLA Ops:
  1.9 33.9 %shard_map.58 = (f32[32,64,128]{2,1,0:T(8,128)S(1)}, f32[256]{0:T(256)S(1)}, f32[4]{0:T(128)S(4)}) custom-call(f32[32,64,128]{2,1,0:T(8,128)} %u_hbm.1, s32[1]{0:T(128)S(6)} %copy.6.first_hbm, s32[1]{0:T(128)S(6)} %copy.7.beyond_hbm), custom_call_target="tpu_custom_call" | custom-call | tf_op jit(solution)/shard_map/pallas_call | solution.py:396
  35.8 1.0 %shard_map.59 = (f32[32,64,128]{2,1,0:T(8,128)}, f32[256]{0:T(256)}, f32[4]{0:T(128)}) custom-call(f32[32,64,128]{2,1,0:T(8,128)S(1)} %get-tuple-element.6.mag, f32[256]{0:T(256)S(1)} %get-tuple-element.7.hist, f32[4]{0:T(128)S(4)} %get-tuple-element.8.stat), custom_call_target="tpu_custom_call" | custom-call | tf_op jit(solution)/shard_map/pallas_call | solution.py:436

commit v5 on v4

--- a/solution.py
+++ b/solution.py
@@ -91,21 +91,6 @@
     ]
     for offset in neighbours:
         signal(hop1, **offset)
-    for m in range(dz // 4):
-        both = []
-        for p in (2 * m, 2 * m + 1):
-            out = jnp.zeros((8, dx), jnp.float32)
-            for j in range(16):
-                cell = ext[4 + 2 * p + j // 8, pl.ds(8 + 8 * (j % 8), 8), :]
-                out = jnp.where(slot == j, pltpu.roll(cell, 8 * j + 4, 1), out)
-            packed[p] = out
-            both.append(out)
-        to_high[m] = jnp.where(left_rim, both[0], pltpu.roll(both[1], 4, 1))
-        to_low[m] = jnp.where(left_rim, pltpu.roll(both[0], dx - 4, 1), both[1])
-    x_rims = [
-        send(4, to_low, from_high, a=-1),
-        send(5, to_high, from_low, a=1),
-    ]
     acc[...] = jnp.zeros_like(acc)
     for copy in edge_loads:
         copy.wait()
@@ -113,7 +98,7 @@
     high_edge = beyond[0].astype(jnp.float32) * 0.5 - 0.5
 
     def classify(square, last, stats):
-        wsum, wmax, wmin = stats
+        wsum, wmax, wmin, wnum = stats
         root = square * (SCALE * SCALE) + 1.0
         magnitude = root * lax.rsqrt(root) - 1.0
         place = jnp.clip(magnitude * (0.5 * BINS / RANGE) - 0.25, 0.0, 0.5 * BINS - 0.5)
@@ -125,6 +110,7 @@
             wsum + value,
             jnp.maximum(wmax, value),
             jnp.minimum(wmin, magnitude - (2.0 * RANGE) * weight),
+            wnum + weight,
         )
         coarse = jnp.floor(low * 0.125)
         fine = low - 8.0 * coarse
@@ -153,6 +139,19 @@
             jnp.concatenate(coarses, axis=1), jnp.concatenate(fines, axis=1),
             (((1,), (1,)), ((), ())), preferred_element_type=jnp.float32,
         )
+
+    def pack():
+        for m in range(dz // 4):
+            both = []
+            for p in (2 * m, 2 * m + 1):
+                out = jnp.zeros((8, dx), jnp.float32)
+                for j in range(16):
+                    cell = ext[4 + 2 * p + j // 8, pl.ds(8 + 8 * (j % 8), 8), :]
+                    out = jnp.where(slot == j, pltpu.roll(cell, 8 * j + 4, 1), out)
+                packed[p] = out
+                both.append(out)
+            to_high[m] = jnp.where(left_rim, both[0], pltpu.roll(both[1], 4, 1))
+            to_low[m] = jnp.where(left_rim, pltpu.roll(both[0], dx - 4, 1), both[1])
 
     def tiles(pairs, stats, fresh):
         fines, coarses = [], []
@@ -189,7 +188,7 @@
     inner = [j for j in range(16) if 0 < j % 8 < 7]
     outer = [j for j in range(16) if not 0 < j % 8 < 7]
     nothing = jnp.zeros((8, dx), jnp.float32)
-    stats = (nothing, nothing, jnp.full((8, dx), 1e30, jnp.float32))
+    stats = (nothing, nothing, jnp.full((8, dx), 1e30, jnp.float32), nothing)
 
     def trips(count_of, pairs, which, stats, fresh):
         step = len(pairs) // count_of
@@ -201,8 +200,12 @@
         )
 
     middle = list(range(2, dz // 2 - 2))
-    ends = [0, 1, dz // 2 - 2, dz // 2 - 1]
-
+
+    pack()
+    x_rims = [
+        send(4, to_low, from_high, a=-1),
+        send(5, to_high, from_low, a=1),
+    ]
     stats = trips(3, middle, inner, stats, True)
 
     pl.semaphore_wait(hop1, 6)
@@ -215,14 +218,19 @@
         signal(far2, c=2)
 
     for copy in y_rims:
-        copy.wait_send()
         copy.wait_recv()
     stats = trips(1, middle, outer, stats, False)
 
-    for copy in z_rims:
-        copy.wait_send()
-        copy.wait_recv()
-    stats = trips(2, ends, list(range(16)), stats, True)
+    turn = (4 - lax.rem(gz, 4)) // 4
+
+    def end_planes(i, stats):
+        end = lax.rem(i + turn, 2)
+        rim = ext.at[pl.ds((4 + dz) * end, 4), rows, :]
+        pltpu.make_async_copy(rim, rim, recv_sem.at[1 - end]).wait()
+        at = (dz // 2 - 2) * end
+        return tiles([(at, range(16)), (at + 1, range(16))], stats, True)
+
+    stats = lax.fori_loop(0, 2, end_planes, stats)
 
     if nz > 4:
         pl.semaphore_wait(near2, 3)
@@ -232,10 +240,10 @@
         signal(far3, c=-4)
         signal(far3, c=4)
 
-    rim_stats = (nothing, nothing, jnp.full((8, dx), 1e30, jnp.float32))
+
+    rim_stats = (nothing, nothing, jnp.full((8, dx), 1e30, jnp.float32), nothing)
 
     for copy in x_rims:
-        copy.wait_send()
         copy.wait_recv()
     fines, coarses = [], []
     for p in range(dz // 2):
@@ -263,6 +271,7 @@
     wsum = rim_stats[0] + jnp.where(rim_lane, 0.0, stats[0])
     wmax = jnp.maximum(rim_stats[1], jnp.where(rim_lane, 0.0, stats[1]))
     wmin = jnp.minimum(rim_stats[2], jnp.where(rim_lane, 1e30, stats[2]))
+    wnum = rim_stats[3] + jnp.where(rim_lane, 0.0, stats[3])
 
     total = acc[...]
     same = (
@@ -293,8 +302,11 @@
     row0, row1 = bin_row(0), bin_row(1)
     lane1 = lane[:1]
     row2 = jnp.where(
-        lane1 == 0, jnp.sum(wsum) * 2.0,
-        jnp.where(lane1 == 1, jnp.max(wmax) * 2.0, jnp.min(wmin) + RANGE),
+        lane1 == 0, jnp.min(wmin) + RANGE,
+        jnp.where(
+            lane1 == 1, jnp.max(wmax) * 2.0,
+            jnp.where(lane1 == 2, jnp.sum(wsum), jnp.sum(wnum)) * 2.0,
+        ),
     )
     msg[0:3, :] = jnp.concatenate([row0, row1, row2], axis=0)
 
@@ -307,7 +319,7 @@
         lane3 = lax.broadcasted_iota(jnp.int32, added.shape, 1)
         row3 = lax.broadcasted_iota(jnp.int32, added.shape, 0)
         return jnp.where(
-            (row3 < 2) | (lane3 == 0), added, jnp.where(lane3 == 1, most, least)
+            (row3 < 2) | (lane3 > 1), added, jnp.where(lane3 == 1, most, least)
         )
 
     def spread_out(peers, slot_ref, send_one, recv_one):
@@ -347,6 +359,8 @@
         return 0
 
     lax.fori_loop(0, dz // 8, unpack, 0)
+    for copy in z_rims + y_rims + x_rims:
+        copy.wait_send()
 
     msg[...] = gathered(nx * nz, plane, plane_send, plane_recv)
     if ny > 4:
@@ -356,17 +370,7 @@
 
     hist_ref[pl.ds(0, 128)] = done[0] * (BINS / cells)
     hist_ref[pl.ds(128, 128)] = done[1] * (BINS / cells)
-    bin_id = lax.broadcasted_iota(jnp.int32, (2, 128), 0) * 128 + lax.broadcasted_iota(
-        jnp.int32, (2, 128), 1
-    )
-    inside = (bin_id >= first[0]) & (bin_id < beyond[0])
-    number = jnp.sum(jnp.where(inside, done[0:2], 0.0))
-    last = done[2:3]
-    total, most, least = (jnp.sum(jnp.where(lane1 == k, last, 0.0)) for k in range(3))
-    stat_ref[0] = least
-    stat_ref[1] = most
-    stat_ref[2] = total * (1.0 / cells)
-    stat_ref[3] = number * (1.0 / cells)
+    stat_ref[...] = jnp.where(lane1 < 2, done[2:3], done[2:3] * (1.0 / cells))[0, :4]
 
 
 def write_out(mag, hist, stat, mag_hbm, hist_hbm, stat_hbm, sems):
@@ -398,13 +402,13 @@
             out_shape=(
                 pltpu.VMEM(u.shape, jnp.float32),
                 pltpu.VMEM((BINS,), jnp.float32),
-                pltpu.SMEM((4,), jnp.float32),
+                pltpu.VMEM((4,), jnp.float32),
             ),
             in_specs=[pl.BlockSpec(memory_space=pltpu.HBM)] * 3,
             out_specs=(
                 pl.BlockSpec(memory_space=pltpu.VMEM),
                 pl.BlockSpec(memory_space=pltpu.VMEM),
-                pl.BlockSpec(memory_space=pltpu.SMEM),
+                pl.BlockSpec(memory_space=pltpu.VMEM),
             ),
             scratch_shapes=[
                 pltpu.VMEM((dz + 8, dy + 16, dx), jnp.float32),
@@ -433,6 +437,7 @@
         )(u, first, beyond)
         mag = pltpu.with_memory_space_constraint(mag, pltpu.VMEM)
         hist = pltpu.with_memory_space_constraint(hist, pltpu.VMEM)
+        stat = pltpu.with_memory_space_constraint(stat, pltpu.VMEM)
         return pl.pallas_call(
             write_out,
             out_shape=(
@@ -443,7 +448,7 @@
             in_specs=[
                 pl.BlockSpec(memory_space=pltpu.VMEM),
                 pl.BlockSpec(memory_space=pltpu.VMEM),
-                pl.BlockSpec(memory_space=pltpu.SMEM),
+                pl.BlockSpec(memory_space=pltpu.VMEM),
             ],
             out_specs=[pl.BlockSpec(memory_space=pltpu.HBM)] * 3,
             scratch_shapes=[pltpu.SemaphoreType.DMA((6,))],

time: 37 us -> 36.4 us (0.984)
  Pallas kernels: 34.9 us -> 34.3 us
    pallas_call x1, Pallas kernels: 33.9 us -> 33.3 us  [on_device(): pl.pallas_call(functools.partial(kernel, sizes, cells), out_shape=(pltpu....]
where the time goes in v5:
time: 36.4 us; the launch traced here: 36.3 us
  Pallas kernels  34.3 us (94%)
  between operations  1.93 us (5%)
    pallas_call x1, Pallas kernels, on_device(): pl.pallas_call(functools.partial(kernel, sizes, cells), out_shape=(pltpu....  33.3 us
    pallas_call x1, Pallas kernels, on_device(): pl.pallas_call(write_out, out_shape=(jax.ShapeDtypeStruct(u.shape, jnp.fl...  1.02 us

profile of v5, /device:TPU:1, one launch (start us, length us, event | category | flops | bytes accessed | tf_op | source)
XLA Modules:
  0.0 36.3 jit_solution(13748016791596807958)
XLA Ops:
  1.9 33.3 %shard_map.58 = (f32[32,64,128]{2,1,0:T(8,128)S(1)}, f32[256]{0:T(256)S(1)}, f32[4]{0:T(128)S(1)}) custom-call(f32[32,64,128]{2,1,0:T(8,128)} %u_hbm.1, s32[1]{0:T(128)S(6)} %copy.6.first_hbm, s32[1]{0:T(128)S(6)} %copy.7.beyond_hbm), custom_call_target="tpu_custom_call" | custom-call | tf_op jit(solution)/shard_map/pallas_call | solution.py:400
  35.2 1.0 %shard_map.59 = (f32[32,64,128]{2,1,0:T(8,128)}, f32[256]{0:T(256)}, f32[4]{0:T(128)}) custom-call(f32[32,64,128]{2,1,0:T(8,128)S(1)} %get-tuple-element.6.mag, f32[256]{0:T(256)S(1)} %get-tuple-element.7.hist, f32[4]{0:T(128)S(1)} %get-tuple-element.8.stat), custom_call_target="tpu_custom_call" | custom-call | tf_op jit(solution)/shard_map/pallas_call | solution.py:441

commit v6 on v5

--- a/solution.py
+++ b/solution.py
@@ -311,11 +311,17 @@
     msg[0:3, :] = jnp.concatenate([row0, row1, row2], axis=0)
 
     def merged(slots, slot_ref):
-        value = slot_ref[0]
-        added, most, least = value, value, value
-        for k in range(1, slots):
-            value = slot_ref[k]
-            added, most, least = added + value, jnp.maximum(most, value), jnp.minimum(least, value)
+        values = [slot_ref[k] for k in range(slots)]
+
+        def tree(combine):
+            level = values
+            while len(level) > 1:
+                level = [combine(x, y) for x, y in zip(level[::2], level[1::2])] + (
+                    level[-1:] if len(level) % 2 else []
+                )
+            return level[0]
+
+        added, most, least = tree(jnp.add), tree(jnp.maximum), tree(jnp.minimum)
         lane3 = lax.broadcasted_iota(jnp.int32, added.shape, 1)
         row3 = lax.broadcasted_iota(jnp.int32, added.shape, 0)
         return jnp.where(
@@ -323,12 +329,12 @@
         )
 
     def spread_out(peers, slot_ref, send_one, recv_one):
-        slot_ref[0] = msg[...]
         for k, offset in enumerate(peers, start=1):
             pltpu.make_async_remote_copy(
                 src_ref=msg, dst_ref=slot_ref.at[k], send_sem=send_one, recv_sem=recv_one,
                 device_id=device(**offset), device_id_type=MESH,
             ).start()
+        slot_ref[0] = msg[...]
 
     def gathered(slots, slot_ref, send_one, recv_one):
         rest = slot_ref.at[pl.ds(1, slots - 1)]

time: 36.4 us -> 36.4 us (level)
  no operation moved by 1% of the time
where the time goes in v6:
time: 36.4 us; the launch traced here: 36.2 us
  Pallas kernels  34.3 us (94%)
  between operations  1.93 us (5%)
    pallas_call x1, Pallas kernels, on_device(): pl.pallas_call(functools.partial(kernel, sizes, cells), out_shape=(pltpu....  33.3 us
    pallas_call x1, Pallas kernels, on_device(): pl.pallas_call(write_out, out_shape=(jax.ShapeDtypeStruct(u.shape, jnp.fl...  1.02 us

profile of v6, /device:TPU:1, one launch (start us, length us, event | category | flops | bytes accessed | tf_op | source)
XLA Modules:
  0.0 36.2 jit_solution(7497564952945771114)
XLA Ops:
  1.9 33.3 %shard_map.58 = (f32[32,64,128]{2,1,0:T(8,128)S(1)}, f32[256]{0:T(256)S(1)}, f32[4]{0:T(128)S(1)}) custom-call(f32[32,64,128]{2,1,0:T(8,128)} %u_hbm.1, s32[1]{0:T(128)S(6)} %copy.6.first_hbm, s32[1]{0:T(128)S(6)} %copy.7.beyond_hbm), custom_call_target="tpu_custom_call" | custom-call | tf_op jit(solution)/shard_map/pallas_call | solution.py:406
  35.2 1.0 %shard_map.59 = (f32[32,64,128]{2,1,0:T(8,128)}, f32[256]{0:T(256)}, f32[4]{0:T(128)}) custom-call(f32[32,64,128]{2,1,0:T(8,128)S(1)} %get-tuple-element.6.mag, f32[256]{0:T(256)S(1)} %get-tuple-element.7.hist, f32[4]{0:T(128)S(1)} %get-tuple-element.8.stat), custom_call_target="tpu_custom_call" | custom-call | tf_op jit(solution)/shard_map/pallas_call | solution.py:447
